TPU v7x, 128 devices: a whole 4x4x4 slice. The times are simulated.
128 devices in a mesh: chan: 4 (over x), rows: 32 (over z, y, core).
Axes of the slice: x: 4, y: 4, z: 4, core: 2. Of those that a mesh axis runs over, the one named last changes fastest.
Arguments:
- residual: float32 [4, 1024, 16384], P('chan', 'rows'), may hold values from -6 to 6
- psf: float32 [4, 2048, 2048], P('chan', 'rows'), may hold values from -2 to 2
- positions: int32 [32, 2], replicated, may hold values from 0 to 15360, as said below
Outputs:
- residual_out: float32 [4, 1024, 16384], P('chan', 'rows')
- normalized: float32 [1024, 16384], P('rows', 'chan')
Inputs may be any that keep to these rules, and one draw needn't show every extreme that they name: positions[k, 0] is a row of the image, 0 to 1023; positions[k, 1] is a column from 1024 to 15360.
All inputs are finite; a program needn't handle non-finite values.
Results may differ from a plain program's by a relative error of at most 0.0001.
Values sent between devices are 32-bit elements; how exact they have to be, the bound alone decides.
A program may use at most 128 MiB of HBM per device.

v0:
```python
import functools

import jax
import jax.numpy as jnp
from jax import lax
from jax.sharding import Mesh
from jax.sharding import PartitionSpec as P

STEPS = 32
ROWS = ("rows_0", "rows_1", "rows_2")
CHAN_ROWS = ("chan", "rows_0", "rows_1", "rows_2")


def by_axis(shard, axes):
    return functools.reduce(lax.psum, axes, shard)


def on_device(residual, psf, positions):
    chan_id = lax.axis_index("chan")
    nchan = lax.axis_size("chan")
    row_id = lax.axis_index(ROWS)
    nrows = lax.axis_size(ROWS)
    slab = residual.shape[1]
    ncols = residual.shape[2]
    own_psf = psf[0]
    shard_rows = own_psf.shape[0]
    patch = own_psf.shape[1]
    half = patch // 2
    first = row_id * slab
    chan_hot = (jnp.arange(nchan) == chan_id).astype(jnp.float32)
    full_psf = lax.all_gather(own_psf, ROWS, axis=0, tiled=True)
    padded_psf = jnp.pad(full_psf, ((slab, slab), (0, 0)))
    zero = jnp.int32(0)

    def subtract(image, row, col, amount):
        offset = first - row + half
        touches = jnp.logical_and(offset > -slab, offset < patch)
        start = jnp.clip(offset + slab, 0, patch + slab)
        psf_rows = lax.dynamic_slice(padded_psf, (start, zero), (slab, patch))
        window = lax.dynamic_slice(image, (zero, col - half), (slab, patch))
        scale = jnp.where(touches, amount, 0.0)
        return lax.dynamic_update_slice(image, window - scale * psf_rows, (zero, col - half))

    image = residual[0]
    peak_rows = positions[:, 0]
    peak_cols = positions[:, 1]
    inside = jnp.logical_and(peak_rows >= first, peak_rows < first + slab)
    local_rows = jnp.clip(peak_rows - first, 0, slab - 1)
    start_values = jnp.where(inside, image[local_rows, peak_cols], 0.0)
    row_offset = peak_rows[:, None] - peak_rows[None, :] + half - row_id * shard_rows
    col_offset = peak_cols[:, None] - peak_cols[None, :] + half
    owned = (row_offset >= 0) & (row_offset < shard_rows) & (col_offset >= 0) & (col_offset < patch)
    couple = own_psf[jnp.clip(row_offset, 0, shard_rows - 1), jnp.clip(col_offset, 0, patch - 1)]
    couple = jnp.where(owned, couple, 0.0)
    start_table, couple_table = (
        by_axis(chan_hot[:, None] * start_values[None, :], CHAN_ROWS),
        by_axis(chan_hot[:, None, None] * couple[None, :, :], CHAN_ROWS),
    )

    def solve(k, amps):
        taken = jnp.sum(amps * lax.dynamic_index_in_dim(couple_table, k, 1, False), axis=1)
        value = lax.dynamic_index_in_dim(start_table, k, 1, False) - taken
        amp = 0.25 * (value + jnp.sum(value) / nchan)
        return lax.dynamic_update_index_in_dim(amps, amp, k, 1)

    amps = lax.fori_loop(0, STEPS, solve, jnp.zeros((nchan, STEPS), jnp.float32))
    own_amps = jnp.sum(chan_hot[:, None] * amps, axis=0)

    def apply(k, image):
        return subtract(image, positions[k, 0], positions[k, 1], own_amps[k])

    image = lax.fori_loop(0, STEPS, apply, image)
    count = slab * nrows * ncols
    parts = lax.psum_scatter(image, "chan", scatter_dimension=1, tiled=True)
    total = by_axis(jnp.sum(parts * parts), CHAN_ROWS)
    normalized = parts * lax.rsqrt(total / count + 1e-06)
    return (image[None], normalized)


def solution(mesh):
    finer = Mesh(
        mesh.devices.reshape(mesh.shape["chan"], 4, 4, 2), ("chan", "rows_0", "rows_1", "rows_2")
    )
    return jax.shard_map(
        on_device,
        mesh=finer,
        in_specs=(P("chan", ROWS, None), P("chan", ROWS, None), P()),
        out_specs=(P("chan", ROWS, None), P(ROWS, "chan")),
        check_vma=False,
    )
```

profile of v0, /device:TPU:1, one launch (start us, length us, event | category | flops | bytes accessed | tf_op | source)
XLA Modules:
  0.0 407.0 jit_solution(14780614954989657997)
XLA Ops:
  7.2 1.6 copy.28
  9.2 8.6 %gather_fusion.1 = f32[1024]{0:T(1024)S(1)} fusion(f32[64,2048]{1,0:T(8,128)S(1)} %bitcast.46, s32[1024]{0:T(1024)S(1)} %reshape.252), kind=kCustom, calls=%fused_computation.1 | custom fusion | bytes 16384 | tf_op jit(solution)/shard_map/gather | solution.py:53
  18.8 16.1 %all-reduce.3 = (f32[4,32]{1,0:T(4,128)S(1)}, f32[4,32,32]{2,0,1:T(4,128)S(1)}) all-reduce(f32[4,32]{1,0:T(4,128)S(1)} %broadcast_multiply_fusion.2, f32[4,32,32]{2,0,1:T(4,128)S(1)} %broadcast_multiply_fusion.1), channel_id=1, replica_groups=mesh['chan'=4,'rows_0'=4,'rows_1'=4,'rows_2'=2] {'chan'}, use_global_device_ids=true, to_apply=%region_4.5 | all-reduce | flops 4224 | bytes 33792 | tf_op jit(solution)/shard_map/psum | solution.py:15
  34.9 15.7 %all-reduce.2 = (f32[4,32]{1,0:T(4,128)S(1)}, f32[4,32,32]{2,0,1:T(4,128)S(1)}) all-reduce(f32[4,32]{1,0:T(4,128)S(1)} %get-tuple-element.307, f32[4,32,32]{2,0,1:T(4,128)S(1)} %get-tuple-element.308), channel_id=1, replica_groups=mesh['chan'=4,'rows_0'=4,'rows_1'=4,'rows_2'=2] {'rows_0'}, use_global_device_ids=true, to_apply=%region_5.6 | all-reduce | flops 4224 | bytes 33792 | tf_op jit(solution)/shard_map/psum | solution.py:15
  50.6 18.6 %all-reduce.1 = (f32[4,32]{1,0:T(4,128)S(1)}, f32[4,32,32]{2,0,1:T(4,128)S(1)}) all-reduce(f32[4,32]{1,0:T(4,128)S(1)} %get-tuple-element.305, f32[4,32,32]{2,0,1:T(4,128)S(1)} %get-tuple-element.306), channel_id=1, replica_groups=mesh['chan'=4,'rows_0'=4,'rows_1'=4,'rows_2'=2] {'rows_1'}, use_global_device_ids=true, to_apply=%region_6.7 | all-reduce | flops 4224 | bytes 33792 | tf_op jit(solution)/shard_map/psum | solution.py:15
  69.2 12.4 %all-reduce.4 = (f32[4,32]{1,0:T(4,128)S(1)}, f32[4,32,32]{2,0,1:T(4,128)S(1)}) all-reduce(f32[4,32]{1,0:T(4,128)S(1)} %get-tuple-element.303, f32[4,32,32]{2,0,1:T(4,128)S(1)} %get-tuple-element.304), channel_id=1, replica_groups=mesh['chan'=4,'rows_0'=4,'rows_1'=4,'rows_2'=2] {'rows_2'}, use_global_device_ids=true, to_apply=%region_7.8 | all-reduce | flops 4224 | bytes 33792 | tf_op jit(solution)/shard_map/psum | solution.py:15
  81.6 57.8 %while.30 = (s32[]{:T(128)}, f32[4,32]{1,0:T(4,128)S(1)}, f32[4,32]{1,0:T(4,128)S(1)}, f32[4,32,32]{2,0,1:T(4,128)S(1)}, s32[]{:T(128)}, /*index=5*/f32[]{:T(128)}, s32[]{:T(128)}) while((s32[]{:T(128)}, f32[4,32]{1,0:T(4,128)S(1)}, f32[4,32]{1,0:T(4,128)S(1)}, f32[4,32,32]{2,0,1:T(4,128)S(1)}, s32[]{:T(128)}, /*index=5*/f32[]{:T(128)}, ...), condition=%wide.region_11.12_spmd, body=%wide.region_8.11_spmd.sunk | while | flops 274 | bytes 2329 | solution.py:66
  139.5 11.7 %pad.4 = f32[2112,2048]{1,0:T(8,128)} pad(f32[2048,2048]{1,0:T(8,128)} %bitcast.50, f32[]{:T(128)} %constant.215.clone.1), padding=32_32x0_0 | pad | bytes 34078724 | tf_op jit(solution)/shard_map/jit(_pad)/pad | solution.py:32
  151.3 182.6 %while.31 = (s32[]{:T(128)}, f32[32,16384]{1,0:T(8,128)S(1)}, s32[32,2]{0,1:T(2,128)S(1)}, s32[]{:T(128)}, f32[32]{0:T(128)S(1)}, /*index=5*/f32[2112,2048]{1,0:...) while((s32[]{:T(128)}, f32[32,16384]{1,0:T(8,128)S(1)}, ...), condition=%wide.region_14.15_spmd, body=%wide.region_13.14_spmd.sunk | while | flops 131087 | bytes 1311065 | solution.py:72
  155.1 1.1 multiply_subtract_fusion.2
  160.8 1.1 multiply_subtract_fusion.2
  172.2 1.1 multiply_subtract_fusion.2
  177.9 1.1 multiply_subtract_fusion.2
  189.3 1.1 multiply_subtract_fusion.2
  206.4 1.1 multiply_subtract_fusion.2
  217.5 1.1 multiply_subtract_fusion.2
  234.5 1.1 multiply_subtract_fusion.2
  257.3 1.1 multiply_subtract_fusion.2
  274.4 1.1 multiply_subtract_fusion.2
  291.5 1.1 multiply_subtract_fusion.2
  297.2 1.1 multiply_subtract_fusion.2
  320.0 1.1 multiply_subtract_fusion.2
  321.1 1.4 dynamic_update_slice.24
  326.4 1.1 multiply_subtract_fusion.2
  333.9 1.3 copy-done.1
  335.2 25.5 %reduce-scatter.2.cloned.1.call-done = f32[32,4096]{1,0:T(8,128)} async-done(((f32[32,16384]{1,0:T(8,128)}), f32[32,4096]{1,0:T(8,128)}) %reduce-scatter.2.cloned.1.call-update) | async-done | bytes 524304 | tf_op jit(solution)/shard_map/reduce_scatter | solution.py:74
  360.8 1.8 multiply_reduce_fusion
  362.5 7.2 %psum.92 = f32[]{:T(128)} all-reduce(f32[]{:T(128)} %multiply_reduce_fusion), channel_id=1, replica_groups=mesh['chan'=4,'rows_0'=4,'rows_1'=4,'rows_2'=2] {'chan'}, use_global_device_ids=true, to_apply=%region_17.18 | all-reduce | flops 1 | bytes 8 | tf_op jit(solution)/shard_map/psum | solution.py:15
  369.7 9.6 %psum.93 = f32[]{:T(128)} all-reduce(f32[]{:T(128)} %psum.92), channel_id=1, replica_groups=mesh['chan'=4,'rows_0'=4,'rows_1'=4,'rows_2'=2] {'rows_0'}, use_global_device_ids=true, to_apply=%region_18.19 | all-reduce | flops 1 | bytes 8 | tf_op jit(solution)/shard_map/psum | solution.py:15
  379.3 8.7 %psum.94 = f32[]{:T(128)} all-reduce(f32[]{:T(128)} %psum.93), channel_id=1, replica_groups=mesh['chan'=4,'rows_0'=4,'rows_1'=4,'rows_2'=2] {'rows_1'}, use_global_device_ids=true, to_apply=%region_19.20 | all-reduce | flops 1 | bytes 8 | tf_op jit(solution)/shard_map/psum | solution.py:15
  388.0 9.5 %psum.95 = f32[]{:T(128)} all-reduce(f32[]{:T(128)} %psum.94), channel_id=1, replica_groups=mesh['chan'=4,'rows_0'=4,'rows_1'=4,'rows_2'=2] {'rows_2'}, use_global_device_ids=true, to_apply=%region_20.21 | all-reduce | flops 1 | bytes 8 | tf_op jit(solution)/shard_map/psum | solution.py:15
  398.2 1.9 broadcast_multiply_fusion
  (327 shorter events, 116.4 us)
Async XLA Ops:
  7.2 2.0 copy-start
  7.2 1.8 copy-start.2
  7.2 132.3 %all-gather.3.cloned.1.call-start = ((), (), s32[]{:S(2)}) async-start(), calls=%async_computation.2 | async-start | bytes 17301504 | tf_op jit(solution)/shard_map/all_gather | solution.py:31
  8.9 351.9 %reduce-scatter.2.cloned.1.call-start = ((), (), s32[]{:S(2)}) async-start(), calls=%async_computation.1 | async-start | bytes 2621440 | tf_op jit(solution)/shard_map/reduce_scatter | solution.py:74
  333.9 1.3 copy-start.1
Sparse Core Ops, SparseCore 0:
  10.3 77.2 all-gather.2
  335.3 25.3 reduce-scatter.1
where the time goes:
time: 411 us; the launch traced here: 407 us
  loops' own time  108 us (26%)
  blocking collectives  97.8 us (24%)
  local copies, waits for them, and re-layouts  93.9 us (23%)
  other arithmetic  66.3 us (16%)
  waiting for transfers between devices  25.6 us (6%)
  between operations  14.9 us (4%)
    psum x8, blocking collectives, by_axis(): return functools.reduce(lax.psum, axes, shard)  97.8 us
    another operation x1, loops' own time, on_device(): image = lax.fori_loop(0, STEPS, apply, image)  85.9 us
    dynamic_slice x64, local copies, waits for them, and re-layouts, apply(): return subtract(image, positions[k, 0], positions[k, 1], own_amps[k])  39.9 us
    sub x32, other arithmetic, subtract(): window - scale * psf_rows  35.8 us
    reduce_scatter x1, waiting for transfers between devices, on_device(): parts = lax.psum_scatter(image, 'chan', scatter_dimension=1, tiled=True)  25.5 us
    another operation x1, loops' own time, on_device(): lax.fori_loop(0, STEPS, solve, jnp.zeros((nchan, STEPS), jnp.float32))  22.5 us
    reduce_sum x32, other arithmetic, solve(): amp = 0.25 * (value + jnp.sum(value) / nchan)  22.1 us
    dynamic_update_slice x32, local copies, waits for them, and re-layouts, subtract(): lax.dynamic_update_slice(image, window - scale * psf_rows, (zero, col - h...  21 us
  transfers between devices with their start and end apart: 2, of which 1 were waited for; matrix products, arithmetic and copies ran while one was open for 11% of the time, Pallas kernels for 0%

commit v1 on v0

v1 whole, which is shorter than its diff:
```python
import functools

import jax
import jax.numpy as jnp
from jax import lax
from jax.experimental import pallas as pl
from jax.experimental.pallas import tpu as pltpu
from jax.sharding import Mesh
from jax.sharding import PartitionSpec as P

STEPS = 32
PAD = 8
LANES = 128
ROWS = ("z", "y", "core")
MESH = pl.DeviceIdType.MESH
F32 = jnp.float32
PIECES = (("z", 1, 0, 3), ("z", -1, 3, 3), ("y", 1, 6, 5), ("y", -1, 11, 5))
HOMES = sorted(((dz, dy) for dz in range(4) for dy in range(4)), key=lambda d: (min(d[0], 4 - d[0]) + min(d[1], 4 - d[1]), d))


def table_kernel(pos, res, psf, own, part, tiles, load_sem, tile_sem):
    unit = 8 * lax.axis_index("z") + 2 * lax.axis_index("y") + lax.axis_index("core")
    slab = res.shape[1]
    rows = own.shape[1] - 2 * PAD
    blocks = own.shape[0]
    half = blocks * LANES // 2
    own_copies = [
        pltpu.make_async_copy(psf.at[0, :, pl.ds(b * LANES, LANES)], own.at[b, pl.ds(PAD, rows)], load_sem.at[b])
        for b in range(blocks)
    ]
    for copy in own_copies:
        copy.start()

    def place(k):
        return pos[k, 0] - unit * slab, pos[k, 1]

    tile_copies = []
    for k in range(STEPS):
        row, col = place(k)
        row = pl.multiple_of(jnp.clip(row, 0, slab - 1) // 8 * 8, 8)
        col = pl.multiple_of(col // LANES * LANES, LANES)
        copy = pltpu.make_async_copy(res.at[0, pl.ds(row, 8), pl.ds(col, LANES)], tiles.at[k], tile_sem.at[k])
        copy.start()
        tile_copies.append(copy)
    for b in range(blocks):
        own[b, :PAD, :] = jnp.zeros((PAD, LANES), F32)
        own[b, PAD + rows :, :] = jnp.zeros((PAD, LANES), F32)
    for copy in own_copies:
        copy.wait()

    wide = lax.broadcasted_iota(jnp.int32, (8, LANES), 1)
    deep = lax.broadcasted_iota(jnp.int32, (8, LANES), 0)

    def placed(tile, base):
        return jnp.where(wide == base + deep, jnp.sum(tile, axis=1, keepdims=True), 0.0)

    def couple(j, total):
        base = LANES // 4 * lax.rem(j, 4)
        for k0 in range(0, STEPS, 8):
            tile = jnp.zeros((8, LANES), F32)
            for s in range(8):
                row = pos[k0 + s, 0] - pos[j, 0] + half - unit * rows
                col = pos[k0 + s, 1] - pos[j, 1] + half
                valid = (row >= 0) & (row < rows) & (col >= 0) & (col < 2 * half)
                col = jnp.clip(col, 0, 2 * half - 1)
                found = own[col // LANES, pl.ds(PAD + jnp.clip(row, 0, rows - 1) - s, 8), :]
                tile = tile + jnp.where((wide == lax.rem(col, LANES)) & (deep == s) & valid, found, 0.0)
            total = total + placed(tile, base + k0)
        return total

    last = STEPS // 4 - 1

    def couple_row(i, carry):
        total = lax.fori_loop(4 * i, 4 * i + 4 - i // last, couple, jnp.zeros((8, LANES), F32))
        part[pl.ds(i, 1), :] = jnp.sum(total, axis=0, keepdims=True)
        return carry

    lax.fori_loop(0, STEPS // 4, couple_row, 0)
    for copy in tile_copies:
        copy.wait()
    total = jnp.zeros((8, LANES), F32)
    for k0 in range(0, STEPS, 8):
        tile = jnp.zeros((8, LANES), F32)
        for s in range(8):
            row, col = place(k0 + s)
            valid = (row >= 0) & (row < slab)
            found = tiles[k0 + s]
            found = jnp.where((wide == lax.rem(col, LANES)) & (deep == lax.rem(row, 8)) & valid, found, 0.0)
            tile = tile + jnp.where(deep == s, jnp.sum(found, axis=0, keepdims=True), 0.0)
        total = total + placed(tile, LANES * 3 // 4 + k0)
    part[last : last + 1, :] = part[last : last + 1, :] + jnp.sum(total, axis=0, keepdims=True)


def peak_table(positions, residual, psf):
    rows, patch = psf.shape[1:]
    sems = pltpu.SemaphoreType.DMA
    return pl.pallas_call(
        table_kernel,
        out_shape=(pltpu.VMEM((patch // LANES, rows + 2 * PAD, LANES), F32), pltpu.VMEM((8, LANES), F32)),
        in_specs=[pl.BlockSpec(memory_space=pltpu.SMEM)] + [pl.BlockSpec(memory_space=pltpu.HBM)] * 2,
        out_specs=(pl.BlockSpec(memory_space=pltpu.VMEM),) * 2,
        scratch_shapes=[pltpu.VMEM((STEPS, 8, LANES), F32), sems((patch // LANES,)), sems((STEPS,))],
        compiler_params=pltpu.CompilerParams(vmem_limit_bytes=8 * 1024 * 1024),
        name="table",
    )(positions, pinned(residual, pltpu.HBM), pinned(psf, pltpu.HBM))


pinned = pltpu.with_memory_space_constraint


def gather_kernel(own, first_part, psf, g, amps, part, got, table, load_sem, send_sem, recv_sem, peer_send, peer_recv, sum_send, sum_recv):
    x, z, y, core = (lax.axis_index(a) for a in ("chan",) + ROWS)
    coord = {"z": z, "y": y, "chan": x, "core": core}
    size = {"z": 4, "y": 4, "chan": 4, "core": 2}
    rows = own.shape[1] - 2 * PAD
    blocks = own.shape[0]

    def device(axis, step):
        return {axis: lax.rem(coord[axis] + step % size[axis], size[axis])}

    barrier = pltpu.get_barrier_semaphore()
    greeted = [("core", 1)] + [(axis, step) for axis in ("y", "z", "chan") for step in (1, 2, 3)]
    for axis, step in greeted:
        pl.semaphore_signal(barrier, inc=1, device_id=device(axis, step), device_id_type=MESH)

    unit = 8 * z + 2 * y + core
    place_copies = [
        pltpu.make_async_copy(psf.at[0, :, pl.ds(b * LANES, LANES)], g.at[b, pl.ds(unit * rows, rows)], load_sem.at[b])
        for b in range(blocks)
    ]
    for copy in place_copies:
        copy.start()
    pl.semaphore_wait(barrier, len(greeted))

    def home(d):
        zh, yh = lax.rem(z + d[0], 4), lax.rem(y + d[1], 4)
        return 4 * zh + yh

    def needed(h, step_z):
        row = lax.rem(z + step_z % 4, 4)
        return jnp.logical_and(h >= 2 * row, h <= 2 * row + 9)

    sends = []

    def forward(d, piece, axis, step, condition):
        first, _, start, count = PIECES[piece]
        rel = list(d)
        rel["zy".index(axis)] = (rel["zy".index(axis)] - step) % 4
        slot = (rel[0] * 4 + rel[1]) * 4 + piece
        dst = g.at[pl.ds(start, count), pl.ds((2 * home(d) + core) * rows, rows)]
        src = own.at[pl.ds(start, count), pl.ds(PAD, rows)] if d == (0, 0) else dst
        copy = pltpu.make_async_remote_copy(src, dst, send_sem.at[len(sends)], recv_sem.at[slot], device_id=device(axis, step), device_id_type=MESH)
        pl.when(condition)(copy.start)
        sends.append((copy, condition))

    def share(d, piece, condition):
        _, _, start, count = PIECES[piece]
        slot = (d[0] * 4 + d[1]) * 4 + piece
        dst = g.at[pl.ds(start, count), pl.ds((2 * home(d) + core) * rows, rows)]
        src = own.at[pl.ds(start, count), pl.ds(PAD, rows)] if d == (0, 0) else dst
        copy = pltpu.make_async_remote_copy(src, dst, peer_send.at[slot], peer_recv.at[slot], device_id=device("core", 1), device_id_type=MESH)
        pl.when(condition)(copy.start)
        return copy

    shares = []

    def arrived(d, piece):
        first, way, start, count = PIECES[piece]
        second = "y" if first == "z" else "z"
        rel = dict(zip("zy", d))
        h = home(d)
        here = needed(h, 0)
        if d != (0, 0):
            slot = (d[0] * 4 + d[1]) * 4 + piece
            dst = g.at[pl.ds(start, count), pl.ds((2 * h + core) * rows, rows)]
            wait = pltpu.make_async_remote_copy(dst, dst, send_sem.at[0], recv_sem.at[slot], device_id=device("core", 1), device_id_type=MESH)
            pl.when(here)(wait.wait_recv)

        def along(axis, step):
            condition = jnp.logical_and(here, needed(h, step)) if axis == "z" else here
            forward(d, piece, axis, step, condition)

        if rel[second] == 0:
            if rel[first] == 0:
                along(first, 1)
                along(first, -1)
            elif rel[first] == -way % 4:
                along(first, way)
            along(second, 1)
            along(second, -1)
        elif rel[second] == -way % 4:
            along(second, way)
        shares.append((share(d, piece, here), here))

    for piece in range(4):
        arrived((0, 0), piece)

    sums = []

    def exchange(axis, value, steps, at):
        copies = []
        for n, step in enumerate(steps):
            copy = pltpu.make_async_remote_copy(
                part.at[value] if value else first_part, got.at[at + n], sum_send.at[at + n], sum_recv.at[at + n], device_id=device(axis, step), device_id_type=MESH
            )
            copies.append(copy)
        return copies

    stages = [("core", (1,), 0), ("y", (1, 2, 3), 1), ("z", (1, 2, 3), 4), ("chan", (3, 2, 1), 7)]
    waves = [[d for d in HOMES if min(d[0], 4 - d[0]) + min(d[1], 4 - d[1]) == n] for n in range(5)]
    todo = [(d, piece) for wave in waves[1:] for d in wave for piece in range(4)]

    pending = []
    taken = 0
    for n, (axis, steps, at) in enumerate(stages):
        copies = exchange(axis, n, steps, at)
        for copy in copies:
            copy.start()
        for d, piece in todo[taken : taken + SHARE_OUT[n]]:
            arrived(d, piece)
        taken += SHARE_OUT[n]
        for copy in copies:
            copy.wait()
        if axis != "chan":
            part[n + 1] = sum((got[at + m] for m in range(len(steps))), part[n] if n else first_part[...])
    tables = [part[3]] + [got[7 + m] for m in range(3)]
    for i in range(STEPS // 4):
        rows_of = jnp.concatenate([t[i : i + 1, :] for t in tables] + [jnp.zeros((4, LANES), F32)], axis=0)
        for m in range(4):
            table[4 * i + m] = rows_of if m == 0 else pltpu.roll(rows_of, LANES - LANES // 4 * m, 1)

    wide = lax.broadcasted_iota(jnp.int32, (8, LANES), 1)

    def solve(j, left):
        value = jnp.sum(jnp.where(wide == j, left, 0.0), axis=1, keepdims=True)
        amp = 0.25 * (value + jnp.sum(value, axis=0, keepdims=True) / 4)
        amps[j] = jnp.broadcast_to(amp[0:1, :], (8, LANES))
        return left - amp * table[j]

    lax.fori_loop(0, STEPS, solve, table[STEPS - 1])

    for d, piece in todo[taken:]:
        arrived(d, piece)
    for copy in place_copies:
        copy.wait()
    for copy, condition in shares:
        pl.when(condition)(copy.wait)
    for copy, condition in sends:
        pl.when(condition)(copy.wait_send)


SHARE_OUT = (0, 8, 8, 8)


def gather(own, part, psf):
    patch = psf.shape[2]
    blocks = patch // LANES
    sems = pltpu.SemaphoreType.DMA
    return pl.pallas_call(
        gather_kernel,
        out_shape=(pltpu.VMEM((blocks, patch, LANES), F32), pltpu.VMEM((STEPS, 8, LANES), F32)),
        in_specs=[pl.BlockSpec(memory_space=pltpu.VMEM)] * 2 + [pl.BlockSpec(memory_space=pltpu.HBM)],
        out_specs=(pl.BlockSpec(memory_space=pltpu.VMEM),) * 2,
        scratch_shapes=[
            pltpu.VMEM((4, 8, LANES), F32),
            pltpu.VMEM((10, 8, LANES), F32),
            pltpu.VMEM((STEPS, 8, LANES), F32),
            sems((blocks,)),
            sems((128,)),
            sems((64,)),
            sems((64,)),
            sems((64,)),
            sems((10,)),
            sems((10,)),
        ],
        compiler_params=pltpu.CompilerParams(collective_id=0, has_side_effects=True, vmem_limit_bytes=8 * 1024 * 1024),
        name="gather",
    )(pinned(own, pltpu.VMEM), pinned(part, pltpu.VMEM), pinned(psf, pltpu.HBM))


def apply_kernel(pos, amps, g, res, out, img, sems):
    load = pltpu.make_async_copy(res.at[0], img, sems.at[0])
    load.start()
    load.wait()
    slab, ncols = img.shape
    blocks = g.shape[0]
    half = blocks * LANES // 2
    first = slab * (8 * lax.axis_index("z") + 2 * lax.axis_index("y") + lax.axis_index("core"))
    lane = lax.broadcasted_iota(jnp.int32, (8, LANES), 1)
    groups = slab // 8

    def step(k, carry):
        start = first - pos[k, 0] + half
        left = pos[k, 1] - half
        block, shift = left // LANES, lax.rem(left, LANES)
        tail = lane >= shift
        amp = amps[k]
        before = [jnp.zeros((8, LANES), F32)] * groups
        terms = []
        for j in range(blocks + 1):
            if j < blocks:
                now = [pltpu.roll(g[j, pl.ds(start + 8 * i, 8), :] * amp, shift, 1) for i in range(groups)]
            else:
                now = [jnp.zeros((8, LANES), F32)] * groups
            terms.append([jnp.where(tail, n, b) for n, b in zip(now, before)])
            before = now
        for j0 in range(0, blocks + 1, 4):
            js = range(j0, min(j0 + 4, blocks + 1))
            cols = [jnp.minimum(block + j, ncols // LANES - 1) if j == blocks else block + j for j in js]
            at = [pl.ds(pl.multiple_of(col * LANES, LANES), LANES) for col in cols]
            old = [[img[8 * i : 8 * i + 8, a] for i in range(groups)] for a in at]
            for j, a, o in zip(js, at, old):
                for i in range(groups):
                    img[8 * i : 8 * i + 8, a] = o[i] - terms[j][i]
        return carry

    lax.fori_loop(0, STEPS, step, 0)
    store = pltpu.make_async_copy(img, out.at[0], sems.at[0])
    store.start()
    store.wait()


def apply_steps(positions, amps, g, residual):
    return pl.pallas_call(
        apply_kernel,
        out_shape=pltpu.HBM(residual.shape, F32),
        in_specs=[pl.BlockSpec(memory_space=pltpu.SMEM)]
        + [pl.BlockSpec(memory_space=pltpu.VMEM)] * 2
        + [pl.BlockSpec(memory_space=pltpu.HBM)],
        out_specs=pl.BlockSpec(memory_space=pltpu.HBM),
        scratch_shapes=[pltpu.VMEM(residual.shape[1:], F32), pltpu.SemaphoreType.DMA((1,))],
        compiler_params=pltpu.CompilerParams(vmem_limit_bytes=8 * 1024 * 1024),
        name="apply",
    )(positions, pinned(amps, pltpu.VMEM), pinned(g, pltpu.VMEM), pinned(residual, pltpu.HBM))


def on_device(residual, psf, positions):
    own, part = peak_table(positions, residual, psf)
    g, amps = gather(own, part, psf)
    image = apply_steps(positions, amps, g, residual)
    count = residual.shape[1] * residual.shape[2] * lax.axis_size(ROWS)
    parts = lax.psum_scatter(image[0], "chan", scatter_dimension=1, tiled=True)
    total = functools.reduce(lax.psum, ("chan",) + ROWS, jnp.sum(parts * parts))
    return image, parts * lax.rsqrt(total / count + 1e-06)


def solution(mesh):
    finer = Mesh(mesh.devices.reshape(mesh.shape["chan"], 4, 4, 2), ("chan",) + ROWS)
    return jax.shard_map(
        on_device,
        mesh=finer,
        in_specs=(P("chan", ROWS, None), P("chan", ROWS, None), P()),
        out_specs=(P("chan", ROWS, None), P(ROWS, "chan")),
        check_vma=False,
    )
```

time: 411 us -> 163 us (0.40)
  loops' own time: 108 us -> 0 us
  local copies, waits for them, and re-layouts: 93.9 us -> 0.76 us
  Pallas kernels: 0 us -> 76 us
  blocking collectives: 97.8 us -> 35 us
  other arithmetic: 66.3 us -> 3.65 us
  waiting for transfers between devices: 25.6 us -> 32.7 us
    another operation x2 -> x0, loops' own time: 108 us -> none  [the longest x1 85.9 us: on_device(): image = lax.fori_loop(0, STEPS, apply, image)]
    pallas_call x0 -> x3, Pallas kernels: none -> 76 us  [the longest x1 52.9 us: gather(): pl.pallas_call(gather_kernel, out_shape=(pltpu.VMEM((blocks, patch, LANES...]
    psum x8 -> x4, blocking collectives: 97.8 us -> 35 us  [on_device(): total = functools.reduce(lax.psum, ('chan',) + ROWS, jnp.sum(parts * parts))]
    dynamic_slice x64 -> x0, local copies, waits for them, and re-layouts: 39.9 us -> none  [apply(): return subtract(image, positions[k, 0], positions[k, 1], own_amps[k])]
    sub x33 -> x0, other arithmetic: 35.8 us -> none  [the longest x32 35.8 us: subtract(): window - scale * psf_rows]
    reduce_sum x66 -> x1, other arithmetic: 27.8 us -> 1.78 us  [on_device(): total = functools.reduce(lax.psum, ('chan',) + ROWS, jnp.sum(parts * parts))]
    dynamic_update_slice x64 -> x0, local copies, waits for them, and re-layouts: 24.1 us -> none  [the longest x32 21 us: subtract(): lax.dynamic_update_slice(image, window - scale * psf_rows, (zero, col - h...]
    pad x1 -> x0, local copies, waits for them, and re-layouts: 11.7 us -> none  [on_device(): padded_psf = jnp.pad(full_psf, ((slab, slab), (0, 0)))]
  transfers between devices with their start and end apart: 2 -> 1, of which waited for: 1 -> 1; matrix products, arithmetic and copies ran while one was open for 11% -> 0% of each run, Pallas kernels for 0% -> 0%
where the time goes in v1:
time: 163 us
  Pallas kernels  76 us (47%)
  blocking collectives  35 us (21%)
  waiting for transfers between devices  32.7 us (20%)
  between operations  14.7 us (9%)
  other arithmetic  3.65 us (2%)
    pallas_call x1, Pallas kernels, gather(): pl.pallas_call(gather_kernel, out_shape=(pltpu.VMEM((blocks, patch, LANES...  52.9 us
    psum x4, blocking collectives, on_device(): total = functools.reduce(lax.psum, ('chan',) + ROWS, jnp.sum(parts * parts))  35 us
    reduce_scatter x1, waiting for transfers between devices, on_device(): parts = lax.psum_scatter(image[0], 'chan', scatter_dimension=1, tiled=True)  32.7 us
    pallas_call x1, Pallas kernels, peak_table(): pl.pallas_call(table_kernel, out_shape=(pltpu.VMEM((patch // LANES, rows...  14.9 us
    pallas_call x1, Pallas kernels, apply_steps(): pl.pallas_call(apply_kernel, out_shape=pltpu.HBM(residual.shape, F32), in...  8.27 us
  transfers between devices with their start and end apart: 1, of which 1 were waited for; matrix products, arithmetic and copies ran while one was open for 0% of the time, Pallas kernels for 0%

profile of v1, /device:TPU:1, one launch (start us, length us, event | category | flops | bytes accessed | tf_op | source)
XLA Modules:
  0.0 163.0 jit_solution(8782866571867568212)
XLA Ops:
  7.2 0.0 reduce-scatter.2.cloned.1.call-start
  7.2 0.8 copy.6.pos
  8.0 14.9 %table.1 = (f32[16,80,128]{2,1,0:T(8,128)S(1)}, f32[8,128]{1,0:T(8,128)S(1)}) custom-call(s32[32,2]{1,0:T(8,128)S(1)} %copy.6.pos, f32[1,32,16384]{2,1,0:T(8,128)} %res.3, f32[1,64,2048]{2,1,0:T(8,128)} %psf.3), custom_call_target="tpu_custom_call" | custom-call | tf_op jit(solution)/shard_map/table/pallas_call | solution.py:97
  22.8 52.9 %gather.1 = (f32[16,2048,128]{2,1,0:T(8,128)S(1)}, f32[32,8,128]{2,1,0:T(8,128)S(1)}) custom-call(f32[16,80,128]{2,1,0:T(8,128)S(1)} %get-tuple-element.6.own, f32[8,128]{1,0:T(8,128)S(1)} %get-tuple-element.7.first_part, f32[1,64,2048]{2,1,0:T(8,128)} %psf.3), custom_call_target="tpu_custom_call" | custom-call | tf_op jit(solution)/shard_map/gather/pallas_call | solution.py:259
  75.7 8.3 %apply.1 = f32[1,32,16384]{2,1,0:T(8,128)} custom-call(s32[32,2]{1,0:T(8,128)S(1)} %copy.6.pos, f32[32,8,128]{2,1,0:T(8,128)S(1)} %get-tuple-element.8.amps, f32[16,2048,128]{2,1,0:T(8,128)S(1)} %get-tuple-element.9.g, f32[1,32,16384]{2,1,0:T(8,128)} %res.3), custom_call_target="tpu_custom_call" | custom-call | tf_op jit(solution)/shard_map/apply/pallas_call | solution.py:324
  84.0 0.0 reduce-scatter.2.cloned.1.call-update
  84.0 32.7 %reduce-scatter.2.cloned.1.call-done = f32[32,4096]{1,0:T(8,128)} async-done(((f32[32,16384]{1,0:T(8,128)}), f32[32,4096]{1,0:T(8,128)}) %reduce-scatter.2.cloned.1.call-update) | async-done | bytes 524304 | tf_op jit(solution)/shard_map/reduce_scatter | solution.py:342
  116.8 1.8 %multiply_reduce_fusion = f32[]{:T(128)} fusion(f32[32,4096]{1,0:T(8,128)} %reduce-scatter.2.cloned.1.call-done), kind=kLoop, calls=%fused_computation | loop fusion | flops 262143 | bytes 524292 | tf_op jit(solution)/shard_map/reduce_sum | solution.py:343
  118.5 7.2 %psum.28 = f32[]{:T(128)} all-reduce(f32[]{:T(128)} %multiply_reduce_fusion), channel_id=1, replica_groups=mesh['chan'=4,'z'=4,'y'=4,'core'=2] {'chan'}, use_global_device_ids=true, to_apply=%region_2.0 | all-reduce | flops 1 | bytes 8 | tf_op jit(solution)/shard_map/psum | solution.py:343
  125.7 9.3 %psum.29 = f32[]{:T(128)} all-reduce(f32[]{:T(128)} %psum.28), channel_id=1, replica_groups=mesh['chan'=4,'z'=4,'y'=4,'core'=2] {'z'}, use_global_device_ids=true, to_apply=%region_3.0 | all-reduce | flops 1 | bytes 8 | tf_op jit(solution)/shard_map/psum | solution.py:343
  135.0 9.4 %psum.30 = f32[]{:T(128)} all-reduce(f32[]{:T(128)} %psum.29), channel_id=1, replica_groups=mesh['chan'=4,'z'=4,'y'=4,'core'=2] {'y'}, use_global_device_ids=true, to_apply=%region_4.0 | all-reduce | flops 1 | bytes 8 | tf_op jit(solution)/shard_map/psum | solution.py:343
  144.3 9.2 %psum.31 = f32[]{:T(128)} all-reduce(f32[]{:T(128)} %psum.30), channel_id=1, replica_groups=mesh['chan'=4,'z'=4,'y'=4,'core'=2] {'core'}, use_global_device_ids=true, to_apply=%region_5.0 | all-reduce | flops 1 | bytes 8 | tf_op jit(solution)/shard_map/psum | solution.py:343
  154.3 1.9 %broadcast_multiply_fusion = f32[32,4096]{1,0:T(8,128)} fusion(f32[32,4096]{1,0:T(8,128)} %reduce-scatter.2.cloned.1.call-done, f32[]{:T(128)S(6)} %rsqrt.3), kind=kLoop, calls=%fused_computation.1 | loop fusion | flops 131072 | bytes 1048580 | tf_op jit(solution)/shard_map/mul | solution.py:344
Async XLA Ops:
  7.2 109.6 %reduce-scatter.2.cloned.1.call-start = ((), (), s32[]{:S(2)}) async-start(), calls=%async_computation.1 | async-start | bytes 2621440 | tf_op jit(solution)/shard_map/reduce_scatter | solution.py:342
Sparse Core Ops, SparseCore 0:
  84.2 32.5 reduce-scatter.1

commit v2 on v1

--- a/solution.py
+++ b/solution.py
@@ -32,13 +32,13 @@
         copy.start()
 
     def place(k):
-        return pos[k, 0] - unit * slab, pos[k, 1]
+        return pos[0, k] - unit * slab, pos[1, k]
 
     tile_copies = []
     for k in range(STEPS):
         row, col = place(k)
-        row = pl.multiple_of(jnp.clip(row, 0, slab - 1) // 8 * 8, 8)
-        col = pl.multiple_of(col // LANES * LANES, LANES)
+        row = pl.multiple_of(jnp.clip(row, 0, slab - 1) & ~7, 8)
+        col = pl.multiple_of(col & ~127, LANES)
         copy = pltpu.make_async_copy(res.at[0, pl.ds(row, 8), pl.ds(col, LANES)], tiles.at[k], tile_sem.at[k])
         copy.start()
         tile_copies.append(copy)
@@ -54,41 +54,44 @@
     def placed(tile, base):
         return jnp.where(wide == base + deep, jnp.sum(tile, axis=1, keepdims=True), 0.0)
 
-    def couple(j, total):
-        base = LANES // 4 * lax.rem(j, 4)
+    def couple(j, carry):
+        base_row = half - unit * rows - pos[0, j]
+        base_col = half - pos[1, j]
+        base = LANES // 4 * (j & 3)
+        at = pl.ds(j >> 2, 1)
         for k0 in range(0, STEPS, 8):
-            tile = jnp.zeros((8, LANES), F32)
-            for s in range(8):
-                row = pos[k0 + s, 0] - pos[j, 0] + half - unit * rows
-                col = pos[k0 + s, 1] - pos[j, 1] + half
-                valid = (row >= 0) & (row < rows) & (col >= 0) & (col < 2 * half)
-                col = jnp.clip(col, 0, 2 * half - 1)
-                found = own[col // LANES, pl.ds(PAD + jnp.clip(row, 0, rows - 1) - s, 8), :]
-                tile = tile + jnp.where((wide == lax.rem(col, LANES)) & (deep == s) & valid, found, 0.0)
-            total = total + placed(tile, base + k0)
-        return total
-
-    last = STEPS // 4 - 1
-
-    def couple_row(i, carry):
-        total = lax.fori_loop(4 * i, 4 * i + 4 - i // last, couple, jnp.zeros((8, LANES), F32))
-        part[pl.ds(i, 1), :] = jnp.sum(total, axis=0, keepdims=True)
+            places = [(pos[0, k0 + s] + base_row, pos[1, k0 + s] + base_col) for s in range(8)]
+            holds = [(row >= 0) & (row < rows) & (col >= 0) & (col < 2 * half) for row, col in places]
+
+            @pl.when((functools.reduce(jnp.logical_or, holds)) & (k0 + 7 > j))
+            def _():
+                tile = jnp.zeros((8, LANES), F32)
+                for s, ((row, col), held) in enumerate(zip(places, holds)):
+                    col = jnp.clip(col, 0, 2 * half - 1)
+                    found = own[col >> 7, pl.ds(PAD + jnp.clip(row, 0, rows - 1) - s, 8), :]
+                    found = jnp.where((wide == jnp.where(held, col & 127, -1)) & (deep == s), found, 0.0)
+                    tile = tile + found
+                part[at, :] = part[at, :] + jnp.sum(placed(tile, base + k0), axis=0, keepdims=True)
+
         return carry
 
-    lax.fori_loop(0, STEPS // 4, couple_row, 0)
+    part[...] = jnp.zeros((8, LANES), F32)
+    lax.fori_loop(0, STEPS - 1, couple, 0)
     for copy in tile_copies:
         copy.wait()
-    total = jnp.zeros((8, LANES), F32)
+    last = STEPS // 4 - 1
     for k0 in range(0, STEPS, 8):
-        tile = jnp.zeros((8, LANES), F32)
-        for s in range(8):
-            row, col = place(k0 + s)
-            valid = (row >= 0) & (row < slab)
-            found = tiles[k0 + s]
-            found = jnp.where((wide == lax.rem(col, LANES)) & (deep == lax.rem(row, 8)) & valid, found, 0.0)
-            tile = tile + jnp.where(deep == s, jnp.sum(found, axis=0, keepdims=True), 0.0)
-        total = total + placed(tile, LANES * 3 // 4 + k0)
-    part[last : last + 1, :] = part[last : last + 1, :] + jnp.sum(total, axis=0, keepdims=True)
+        places = [place(k0 + s) for s in range(8)]
+        holds = [(row >= 0) & (row < slab) for row, _ in places]
+
+        @pl.when(functools.reduce(jnp.logical_or, holds))
+        def _():
+            tile = jnp.zeros((8, LANES), F32)
+            for s, ((row, col), held) in enumerate(zip(places, holds)):
+                found = jnp.where((wide == (col & 127)) & (deep == jnp.where(held, row & 7, -1)), tiles[k0 + s], 0.0)
+                tile = tile + jnp.where(deep == s, jnp.sum(found, axis=0, keepdims=True), 0.0)
+            found = jnp.sum(placed(tile, LANES * 3 // 4 + k0), axis=0, keepdims=True)
+            part[last : last + 1, :] = part[last : last + 1, :] + found
 
 
 def peak_table(positions, residual, psf):
@@ -108,7 +111,7 @@
 pinned = pltpu.with_memory_space_constraint
 
 
-def gather_kernel(own, first_part, psf, g, amps, part, got, table, load_sem, send_sem, recv_sem, peer_send, peer_recv, sum_send, sum_recv):
+def gather_kernel(own, first_part, psf, res, g, amps, img, part, got, table, load_sem, send_sem, recv_sem, peer_send, peer_recv, sum_send, sum_recv):
     x, z, y, core = (lax.axis_index(a) for a in ("chan",) + ROWS)
     coord = {"z": z, "y": y, "chan": x, "core": core}
     size = {"z": 4, "y": 4, "chan": 4, "core": 2}
@@ -128,6 +131,7 @@
         pltpu.make_async_copy(psf.at[0, :, pl.ds(b * LANES, LANES)], g.at[b, pl.ds(unit * rows, rows)], load_sem.at[b])
         for b in range(blocks)
     ]
+    place_copies.append(pltpu.make_async_copy(res.at[0], img, load_sem.at[blocks]))
     for copy in place_copies:
         copy.start()
     pl.semaphore_wait(barrier, len(greeted))
@@ -252,20 +256,20 @@
 SHARE_OUT = (0, 8, 8, 8)
 
 
-def gather(own, part, psf):
+def gather(own, part, psf, residual):
     patch = psf.shape[2]
     blocks = patch // LANES
     sems = pltpu.SemaphoreType.DMA
     return pl.pallas_call(
         gather_kernel,
-        out_shape=(pltpu.VMEM((blocks, patch, LANES), F32), pltpu.VMEM((STEPS, 8, LANES), F32)),
-        in_specs=[pl.BlockSpec(memory_space=pltpu.VMEM)] * 2 + [pl.BlockSpec(memory_space=pltpu.HBM)],
-        out_specs=(pl.BlockSpec(memory_space=pltpu.VMEM),) * 2,
+        out_shape=(pltpu.VMEM((blocks, patch, LANES), F32), pltpu.VMEM((STEPS, 8, LANES), F32), pltpu.VMEM(residual.shape[1:], F32)),
+        in_specs=[pl.BlockSpec(memory_space=pltpu.VMEM)] * 2 + [pl.BlockSpec(memory_space=pltpu.HBM)] * 2,
+        out_specs=(pl.BlockSpec(memory_space=pltpu.VMEM),) * 3,
         scratch_shapes=[
             pltpu.VMEM((4, 8, LANES), F32),
             pltpu.VMEM((10, 8, LANES), F32),
             pltpu.VMEM((STEPS, 8, LANES), F32),
-            sems((blocks,)),
+            sems((blocks + 1,)),
             sems((128,)),
             sems((64,)),
             sems((64,)),
@@ -275,13 +279,10 @@
         ],
         compiler_params=pltpu.CompilerParams(collective_id=0, has_side_effects=True, vmem_limit_bytes=8 * 1024 * 1024),
         name="gather",
-    )(pinned(own, pltpu.VMEM), pinned(part, pltpu.VMEM), pinned(psf, pltpu.HBM))
-
-
-def apply_kernel(pos, amps, g, res, out, img, sems):
-    load = pltpu.make_async_copy(res.at[0], img, sems.at[0])
-    load.start()
-    load.wait()
+    )(pinned(own, pltpu.VMEM), pinned(part, pltpu.VMEM), pinned(psf, pltpu.HBM), pinned(residual, pltpu.HBM))
+
+
+def apply_kernel(pos, amps, g, given, img):
     slab, ncols = img.shape
     blocks = g.shape[0]
     half = blocks * LANES // 2
@@ -290,9 +291,9 @@
     groups = slab // 8
 
     def step(k, carry):
-        start = first - pos[k, 0] + half
-        left = pos[k, 1] - half
-        block, shift = left // LANES, lax.rem(left, LANES)
+        start = first - pos[0, k] + half
+        left = pos[1, k] - half
+        block, shift = left >> 7, left & 127
         tail = lane >= shift
         amp = amps[k]
         before = [jnp.zeros((8, LANES), F32)] * groups
@@ -315,33 +316,158 @@
         return carry
 
     lax.fori_loop(0, STEPS, step, 0)
-    store = pltpu.make_async_copy(img, out.at[0], sems.at[0])
-    store.start()
-    store.wait()
-
-
-def apply_steps(positions, amps, g, residual):
+
+
+def apply_steps(positions, amps, g, image):
     return pl.pallas_call(
         apply_kernel,
-        out_shape=pltpu.HBM(residual.shape, F32),
-        in_specs=[pl.BlockSpec(memory_space=pltpu.SMEM)]
-        + [pl.BlockSpec(memory_space=pltpu.VMEM)] * 2
-        + [pl.BlockSpec(memory_space=pltpu.HBM)],
-        out_specs=pl.BlockSpec(memory_space=pltpu.HBM),
-        scratch_shapes=[pltpu.VMEM(residual.shape[1:], F32), pltpu.SemaphoreType.DMA((1,))],
+        out_shape=pltpu.VMEM(image.shape, F32),
+        in_specs=[pl.BlockSpec(memory_space=pltpu.SMEM)] + [pl.BlockSpec(memory_space=pltpu.VMEM)] * 3,
+        out_specs=pl.BlockSpec(memory_space=pltpu.VMEM),
+        input_output_aliases={3: 0},
         compiler_params=pltpu.CompilerParams(vmem_limit_bytes=8 * 1024 * 1024),
         name="apply",
-    )(positions, pinned(amps, pltpu.VMEM), pinned(g, pltpu.VMEM), pinned(residual, pltpu.HBM))
+    )(positions, *(pinned(a, pltpu.VMEM) for a in (amps, g, image)))
+
+
+SPLIT = 4
+
+
+def reduce_kernel(img, parts, scale, far, near, sums, squares, got, far_send, far_recv, near_send, near_recv, sums_send, sums_recv, sq_send, sq_recv):
+    x, z, y, core = (lax.axis_index(a) for a in ("chan",) + ROWS)
+    half, width = img.shape[0] // 2, parts.shape[1]
+    piece = width // SPLIT
+
+    close = [(dx, dc) for dc in range(2) for dx in range(4) if (dx, dc) != (0, 0)]
+    plane = [(dz, dy) for dz in range(4) for dy in range(4) if (dz, dy) != (0, 0)]
+
+    def near_id(dx, dc):
+        return {"chan": (x + dx) & 3, "core": (core + dc) & 1}
+
+    def plane_id(dz, dy):
+        return {"z": (z + dz) & 3, "y": (y + dy) & 3}
+
+    peers = [near_id(*d) for d in close] + [plane_id(*d) for d in plane]
+    barrier = pltpu.get_barrier_semaphore()
+    for peer in peers:
+        pl.semaphore_signal(barrier, inc=1, device_id=peer, device_id_type=MESH)
+    pl.semaphore_wait(barrier, len(peers))
+
+    def cols(chunk, q):
+        return pl.ds(pl.multiple_of(((x + chunk) & 3) * width + q * piece, piece), piece)
+
+    def rows(which):
+        return pl.ds(which * half, half)
+
+    def send(src, dst, n, q, sems, way):
+        copy = pltpu.make_async_remote_copy(
+            src, dst.at[n, :, pl.ds(q * piece, piece)], sems[0].at[n * SPLIT + q], sems[1].at[n * SPLIT + q],
+            device_id={"chan": (x + way) & 3}, device_id_type=MESH,
+        )
+        copy.start()
+        return copy
+
+    ways = (1, -1)
+    fars, nears, lasts = {}, {}, {}
+    for q in range(SPLIT):
+        for n, way in enumerate(ways):
+            fars[n, q] = send(img.at[rows(1 - n), cols(2, q)], far, n, q, (far_send, far_recv), way)
+    for q in range(SPLIT):
+        for n, way in enumerate(ways):
+            nears[n, q] = send(img.at[rows(n), cols(way, q)], near, n, q, (near_send, near_recv), way)
+    for q in range(SPLIT):
+        for n, way in enumerate(ways):
+            fars[n, q].wait_recv()
+            at = pl.ds(q * piece, piece)
+            far[n, :, at] = far[n, :, at] + img[rows(1 - n), cols(way, q)]
+            lasts[n, q] = send(far.at[n, :, at], sums, n, q, (sums_send, sums_recv), way)
+    total = jnp.zeros((8, LANES), F32)
+    for q in range(SPLIT):
+        at = pl.ds(q * piece, piece)
+        for n in range(2):
+            nears[n, q].wait_recv()
+            parts[rows(n), at] = img[rows(n), cols(0, q)] + near[n, :, at]
+    for q in range(SPLIT):
+        at = pl.ds(q * piece, piece)
+        for n in range(2):
+            lasts[n, q].wait_recv()
+            value = parts[rows(1 - n), at] + sums[n, :, at]
+            parts[rows(1 - n), at] = value
+            square = value * value
+            for i in range(half // 8):
+                for t in range(piece // LANES):
+                    total = total + square[8 * i : 8 * i + 8, LANES * t : LANES * (t + 1)]
+
+    squares[0] = total
+    done = []
+    for stage, ids, start in ((0, peers[: len(close)], 0), (1, peers[len(close) :], len(close))):
+        copies = [
+            pltpu.make_async_remote_copy(squares.at[stage], got.at[start + i], sq_send.at[start + i], sq_recv.at[start + i], device_id=peer, device_id_type=MESH)
+            for i, peer in enumerate(ids)
+        ]
+        for copy in copies:
+            copy.start()
+        for copy in copies:
+            copy.wait_recv()
+        done += copies
+        squares[stage + 1] = sum((got[start + i] for i in range(len(ids))), squares[stage])
+    total = jnp.sum(jnp.sum(squares[2], axis=1, keepdims=True), axis=0, keepdims=True)
+    count = img.shape[0] * img.shape[1] * 32
+    scale[...] = jnp.broadcast_to(lax.rsqrt(total / count + 1e-06), (8, LANES))
+    for copy in list(fars.values()) + list(nears.values()) + list(lasts.values()) + done:
+        copy.wait_send()
+
+
+def reduce_channels(image):
+    slab, ncols = image.shape
+    width = ncols // 4
+    sems = pltpu.SemaphoreType.DMA
+    return pl.pallas_call(
+        reduce_kernel,
+        out_shape=(pltpu.VMEM((slab, width), F32), pltpu.VMEM((8, LANES), F32)),
+        in_specs=[pl.BlockSpec(memory_space=pltpu.VMEM)],
+        out_specs=(pl.BlockSpec(memory_space=pltpu.VMEM),) * 2,
+        scratch_shapes=[pltpu.VMEM((2, slab // 2, width), F32)] * 3
+        + [pltpu.VMEM((3, 8, LANES), F32), pltpu.VMEM((22, 8, LANES), F32)]
+        + [sems((2 * SPLIT,))] * 6
+        + [sems((22,))] * 2,
+        compiler_params=pltpu.CompilerParams(collective_id=1, has_side_effects=True, vmem_limit_bytes=8 * 1024 * 1024),
+        name="reduce",
+    )(pinned(image, pltpu.VMEM))
+
+
+def write_kernel(img, parts, scale, image_out, normal_out, normal, sems):
+    copies = [pltpu.make_async_copy(img, image_out.at[0], sems.at[0])]
+    copies[0].start()
+    piece = parts.shape[1] // 4
+    for q in range(4):
+        at = pl.ds(q * piece, piece)
+        normal[:, at] = parts[:, at] * scale[0:1, 0:1]
+        copies.append(pltpu.make_async_copy(normal.at[:, at], normal_out.at[:, at], sems.at[q + 1]))
+        copies[-1].start()
+    for copy in copies:
+        copy.wait()
+
+
+def write(image, parts, scale):
+    return pl.pallas_call(
+        write_kernel,
+        out_shape=(pltpu.HBM((1,) + image.shape, F32), pltpu.HBM(parts.shape, F32)),
+        in_specs=[pl.BlockSpec(memory_space=pltpu.VMEM)] * 3,
+        out_specs=(pl.BlockSpec(memory_space=pltpu.HBM),) * 2,
+        scratch_shapes=[pltpu.VMEM(parts.shape, F32), pltpu.SemaphoreType.DMA((5,))],
+        compiler_params=pltpu.CompilerParams(vmem_limit_bytes=8 * 1024 * 1024),
+        name="write",
+    )(*(pinned(a, pltpu.VMEM) for a in (image, parts, scale)))
 
 
 def on_device(residual, psf, positions):
+    positions = positions.T
     own, part = peak_table(positions, residual, psf)
-    g, amps = gather(own, part, psf)
-    image = apply_steps(positions, amps, g, residual)
-    count = residual.shape[1] * residual.shape[2] * lax.axis_size(ROWS)
-    parts = lax.psum_scatter(image[0], "chan", scatter_dimension=1, tiled=True)
-    total = functools.reduce(lax.psum, ("chan",) + ROWS, jnp.sum(parts * parts))
-    return image, parts * lax.rsqrt(total / count + 1e-06)
+    g, amps, image = gather(own, part, psf, residual)
+    image = apply_steps(positions, amps, g, image)
+    parts, scale = reduce_channels(image)
+    return write(image, parts, scale)
 
 
 def solution(mesh):

time: 163 us -> 107 us (0.66)
  blocking collectives: 35 us -> 0 us
  waiting for transfers between devices: 32.7 us -> 0 us
  Pallas kernels: 76 us -> 105 us
  between operations: 14.7 us -> 0.67 us
  other arithmetic: 3.65 us -> 0 us
    pallas_call x1 -> x3, Pallas kernels: 8.27 us -> 44 us  [the longest x1 37.4 us: reduce_channels(): pl.pallas_call(reduce_kernel, out_shape=(pltpu.VMEM((slab, width), F32),...]
    psum x4 -> x0, blocking collectives: 35 us -> none  [on_device(): total = functools.reduce(lax.psum, ('chan',) + ROWS, jnp.sum(parts * parts))]
    reduce_scatter x1 -> x0, waiting for transfers between devices: 32.7 us -> none  [on_device(): parts = lax.psum_scatter(image[0], 'chan', scatter_dimension=1, tiled=True)]
    pallas_call x1, Pallas kernels: 14.9 us -> 8.28 us  [peak_table(): pl.pallas_call(table_kernel, out_shape=(pltpu.VMEM((patch // LANES, rows...]
    mul x1 -> x0, other arithmetic: 1.87 us -> none  [on_device(): return (image, parts * lax.rsqrt(total / count + 1e-06))]
    reduce_sum x1 -> x0, other arithmetic: 1.78 us -> none  [on_device(): total = functools.reduce(lax.psum, ('chan',) + ROWS, jnp.sum(parts * parts))]
  transfers between devices with their start and end apart: 1 -> 0, of which waited for: 1 -> 0; matrix products, arithmetic and copies ran while one was open for 0% -> 0% of each run, Pallas kernels for 0% -> 0%
where the time goes in v2:
time: 107 us
  Pallas kernels  105 us (98%)
    pallas_call x1, Pallas kernels, gather(): pl.pallas_call(gather_kernel, out_shape=(pltpu.VMEM((blocks, patch, LANES...  52.9 us
    pallas_call x1, Pallas kernels, reduce_channels(): pl.pallas_call(reduce_kernel, out_shape=(pltpu.VMEM((slab, width), F32),...  37.4 us
    pallas_call x1, Pallas kernels, peak_table(): pl.pallas_call(table_kernel, out_shape=(pltpu.VMEM((patch // LANES, rows...  8.28 us
    pallas_call x1, Pallas kernels, apply_steps(): pl.pallas_call(apply_kernel, out_shape=pltpu.VMEM(image.shape, F32), in_s...  5.08 us

profile of v2, /device:TPU:1, one launch (start us, length us, event | category | flops | bytes accessed | tf_op | source)
XLA Modules:
  0.0 106.5 jit_solution(5340358660659807853)
XLA Ops:
  0.6 0.0 copy-start
  0.6 0.7 copy-done
  1.3 8.3 %table.1 = (f32[16,80,128]{2,1,0:T(8,128)S(1)}, f32[8,128]{1,0:T(8,128)S(1)}) custom-call(s32[2,32]{1,0:T(2,128)S(1)} %bitcast.1, f32[1,32,16384]{2,1,0:T(8,128)} %res.3, f32[1,64,2048]{2,1,0:T(8,128)} %psf.3), custom_call_target="tpu_custom_call" | custom-call | tf_op jit(solution)/shard_map/table/pallas_call | solution.py:100
  9.6 52.9 %gather.1 = (f32[16,2048,128]{2,1,0:T(8,128)S(1)}, f32[32,8,128]{2,1,0:T(8,128)S(1)}, f32[32,16384]{1,0:T(8,128)S(1)}) custom-call(f32[16,80,128]{2,1,0:T(8,128)S(1)} %get-tuple-element.9.own, f32[8,128]{1,0:T(8,128)S(1)} %get-tuple-element.10.first_part, f32[1,64,2048]{2,1,0:T(8,128)} %psf.3, f32[1,32,16384]{2,1,0:T(8,128)} %res.3), custom_call_target="tpu_custom_call" | custom-call | tf_op jit(solution)/shard_map/gather/pallas_call | solution.py:263
  62.5 5.1 %apply.1.img = f32[32,16384]{1,0:T(8,128)S(1)} custom-call(s32[2,32]{1,0:T(2,128)S(1)} %bitcast.2, f32[32,8,128]{2,1,0:T(8,128)S(1)} %get-tuple-element.11.amps, f32[16,2048,128]{2,1,0:T(8,128)S(1)} %get-tuple-element.12.g, f32[32,16384]{1,0:T(8,128)S(1)} %get-tuple-element.13.given), custom_call_target="tpu_custom_call", output_to_operand_aliasing={{}: (3, {})} | custom-call | tf_op jit(solution)/shard_map/apply/pallas_call | solution.py:322
  67.6 37.4 %reduce.1 = (f32[32,4096]{1,0:T(8,128)S(1)}, f32[8,128]{1,0:T(8,128)S(1)}) custom-call(f32[32,16384]{1,0:T(8,128)S(1)} %apply.1.img), custom_call_target="tpu_custom_call" | custom-call | tf_op jit(solution)/shard_map/reduce/pallas_call | solution.py:425
  105.0 1.5 %write.1 = (f32[1,32,16384]{2,1,0:T(8,128)}, f32[32,4096]{1,0:T(8,128)}) custom-call(f32[32,16384]{1,0:T(8,128)S(1)} %apply.1.img, f32[32,4096]{1,0:T(8,128)S(1)} %get-tuple-element.14.parts, f32[8,128]{1,0:T(8,128)S(1)} %get-tuple-element.15.scale), custom_call_target="tpu_custom_call" | custom-call | tf_op jit(solution)/shard_map/write/pallas_call | solution.py:453
Async XLA Ops:
  0.6 0.7 copy-start

commit v3 on v2

--- a/solution.py
+++ b/solution.py
@@ -14,8 +14,30 @@
 ROWS = ("z", "y", "core")
 MESH = pl.DeviceIdType.MESH
 F32 = jnp.float32
-PIECES = (("z", 1, 0, 3), ("z", -1, 3, 3), ("y", 1, 6, 5), ("y", -1, 11, 5))
-HOMES = sorted(((dz, dy) for dz in range(4) for dy in range(4)), key=lambda d: (min(d[0], 4 - d[0]) + min(d[1], 4 - d[1]), d))
+PIECES = (("z", 1, 0, 4), ("z", -1, 4, 4), ("y", 1, 8, 4), ("y", -1, 12, 4))
+ONE, TWO = (1, 3), (2,)
+ZY, YZ = (0, 1), (2, 3)
+
+
+def order():
+    def both(firsts, seconds):
+        return [
+            item
+            for f in firsts
+            for s in seconds
+            for half in range(2)
+            for item in (((f, s), ZY[half]), ((s, f), YZ[half]))
+        ]
+
+    return [
+        both(ONE, (0,)),
+        both((0,), ONE),
+        both(TWO, (0,)),
+        both(ONE, ONE),
+        both((0,), TWO),
+        both(TWO, ONE),
+        both(ONE, TWO) + both(TWO, TWO),
+    ]
 
 
 def table_kernel(pos, res, psf, own, part, tiles, load_sem, tile_sem):
@@ -24,6 +46,7 @@
     rows = own.shape[1] - 2 * PAD
     blocks = own.shape[0]
     half = blocks * LANES // 2
+    assert (rows, half) == (64, 1024)
     own_copies = [
         pltpu.make_async_copy(psf.at[0, :, pl.ds(b * LANES, LANES)], own.at[b, pl.ds(PAD, rows)], load_sem.at[b])
         for b in range(blocks)
@@ -54,29 +77,26 @@
     def placed(tile, base):
         return jnp.where(wide == base + deep, jnp.sum(tile, axis=1, keepdims=True), 0.0)
 
-    def couple(j, carry):
-        base_row = half - unit * rows - pos[0, j]
-        base_col = half - pos[1, j]
-        base = LANES // 4 * (j & 3)
-        at = pl.ds(j >> 2, 1)
-        for k0 in range(0, STEPS, 8):
-            places = [(pos[0, k0 + s] + base_row, pos[1, k0 + s] + base_col) for s in range(8)]
-            holds = [(row >= 0) & (row < rows) & (col >= 0) & (col < 2 * half) for row, col in places]
-
-            @pl.when((functools.reduce(jnp.logical_or, holds)) & (k0 + 7 > j))
+    part[...] = jnp.zeros((8, LANES), F32)
+    for k0 in range(0, STEPS, 8):
+        peaks = [(pos[0, k0 + s] + half - unit * rows, pos[1, k0 + s] + half) for s in range(8)]
+
+        def couple(j, carry):
+            places = [(row - pos[0, j], col - pos[1, j]) for row, col in peaks]
+            away = [lax.shift_right_logical(row, 6) | lax.shift_right_logical(col, 11) for row, col in places]
+
+            @pl.when(functools.reduce(jnp.minimum, away) == 0)
             def _():
                 tile = jnp.zeros((8, LANES), F32)
-                for s, ((row, col), held) in enumerate(zip(places, holds)):
-                    col = jnp.clip(col, 0, 2 * half - 1)
-                    found = own[col >> 7, pl.ds(PAD + jnp.clip(row, 0, rows - 1) - s, 8), :]
-                    found = jnp.where((wide == jnp.where(held, col & 127, -1)) & (deep == s), found, 0.0)
-                    tile = tile + found
-                part[at, :] = part[at, :] + jnp.sum(placed(tile, base + k0), axis=0, keepdims=True)
-
-        return carry
-
-    part[...] = jnp.zeros((8, LANES), F32)
-    lax.fori_loop(0, STEPS - 1, couple, 0)
+                for s, ((row, col), far) in enumerate(zip(places, away)):
+                    found = own[(col >> 7) & 15, pl.ds(PAD + (row & 63) - s, 8), :]
+                    tile = tile + jnp.where((wide == jnp.where(far == 0, col & 127, -1)) & (deep == s), found, 0.0)
+                at = pl.ds(j >> 2, 1)
+                part[at, :] = part[at, :] + jnp.sum(placed(tile, LANES // 4 * (j & 3) + k0), axis=0, keepdims=True)
+
+            return carry
+
+        lax.fori_loop(0, min(k0 + 7, STEPS - 1), couple, 0)
     for copy in tile_copies:
         copy.wait()
     last = STEPS // 4 - 1
@@ -168,7 +188,7 @@
 
     shares = []
 
-    def arrived(d, piece):
+    def arrived(d, piece, phase=None):
         first, way, start, count = PIECES[piece]
         second = "y" if first == "z" else "z"
         rel = dict(zip("zy", d))
@@ -180,24 +200,32 @@
             wait = pltpu.make_async_remote_copy(dst, dst, send_sem.at[0], recv_sem.at[slot], device_id=device("core", 1), device_id_type=MESH)
             pl.when(here)(wait.wait_recv)
 
-        def along(axis, step):
-            condition = jnp.logical_and(here, needed(h, step)) if axis == "z" else here
+        def along(axis, step, also=True):
+            condition = jnp.logical_and(jnp.logical_and(here, needed(h, step)), also) if axis == "z" else here
             forward(d, piece, axis, step, condition)
 
-        if rel[second] == 0:
-            if rel[first] == 0:
-                along(first, 1)
-                along(first, -1)
-            elif rel[first] == -way % 4:
-                along(first, way)
+        def relay(axis):
+            if axis == "y":
+                if rel["y"] == -way % 4:
+                    along("y", way)
+            elif rel["z"] == 3:
+                along("z", 1, lax.rem(z, 4) == 3)
+            elif rel["z"] == 1:
+                along("z", -1, lax.rem(z, 4) == 0)
+
+        if d == (0, 0):
+            for axis in (first, second) if phase is None else ((first,), (second,))[phase]:
+                along(axis, 1)
+                along(axis, -1)
+            if phase == 0:
+                return
+        elif rel[second] == 0:
+            relay(first)
             along(second, 1)
             along(second, -1)
-        elif rel[second] == -way % 4:
-            along(second, way)
+        else:
+            relay(second)
         shares.append((share(d, piece, here), here))
-
-    for piece in range(4):
-        arrived((0, 0), piece)
 
     sums = []
 
@@ -210,23 +238,28 @@
             copies.append(copy)
         return copies
 
+    waves = order()
     stages = [("core", (1,), 0), ("y", (1, 2, 3), 1), ("z", (1, 2, 3), 4), ("chan", (3, 2, 1), 7)]
-    waves = [[d for d in HOMES if min(d[0], 4 - d[0]) + min(d[1], 4 - d[1]) == n] for n in range(5)]
-    todo = [(d, piece) for wave in waves[1:] for d in wave for piece in range(4)]
-
-    pending = []
-    taken = 0
+    after = ([], waves[0], waves[1] + waves[2], waves[3])
     for n, (axis, steps, at) in enumerate(stages):
         copies = exchange(axis, n, steps, at)
         for copy in copies:
             copy.start()
-        for d, piece in todo[taken : taken + SHARE_OUT[n]]:
+        if n == 0:
+            for piece in range(4):
+                arrived((0, 0), piece, 0)
+        if n == 1:
+            for piece in range(4):
+                arrived((0, 0), piece, 1)
+        for d, piece in after[n]:
             arrived(d, piece)
-        taken += SHARE_OUT[n]
         for copy in copies:
             copy.wait()
         if axis != "chan":
             part[n + 1] = sum((got[at + m] for m in range(len(steps))), part[n] if n else first_part[...])
+    for wave in waves[4:6]:
+        for d, piece in wave:
+            arrived(d, piece)
     tables = [part[3]] + [got[7 + m] for m in range(3)]
     for i in range(STEPS // 4):
         rows_of = jnp.concatenate([t[i : i + 1, :] for t in tables] + [jnp.zeros((4, LANES), F32)], axis=0)
@@ -243,7 +276,7 @@
 
     lax.fori_loop(0, STEPS, solve, table[STEPS - 1])
 
-    for d, piece in todo[taken:]:
+    for d, piece in waves[6]:
         arrived(d, piece)
     for copy in place_copies:
         copy.wait()
@@ -251,9 +284,6 @@
         pl.when(condition)(copy.wait)
     for copy, condition in sends:
         pl.when(condition)(copy.wait_send)
-
-
-SHARE_OUT = (0, 8, 8, 8)
 
 
 def gather(own, part, psf, residual):

time: 107 us -> 93.6 us (0.87)
  Pallas kernels: 105 us -> 92 us
    pallas_call x1, Pallas kernels: 52.9 us -> 45.8 us  [gather(): pl.pallas_call(gather_kernel, out_shape=(pltpu.VMEM((blocks, patch, LANES...]
    pallas_call x1, Pallas kernels: 37.4 us -> 34 us  [reduce_channels(): pl.pallas_call(reduce_kernel, out_shape=(pltpu.VMEM((slab, width), F32),...]
    pallas_call x1, Pallas kernels: 8.28 us -> 5.56 us  [peak_table(): pl.pallas_call(table_kernel, out_shape=(pltpu.VMEM((patch // LANES, rows...]
where the time goes in v3:
time: 93.6 us; the launch traced here: 93.3 us
  Pallas kernels  92 us (98%)
    pallas_call x1, Pallas kernels, gather(): pl.pallas_call(gather_kernel, out_shape=(pltpu.VMEM((blocks, patch, LANES...  45.8 us
    pallas_call x1, Pallas kernels, reduce_channels(): pl.pallas_call(reduce_kernel, out_shape=(pltpu.VMEM((slab, width), F32),...  34 us
    pallas_call x1, Pallas kernels, peak_table(): pl.pallas_call(table_kernel, out_shape=(pltpu.VMEM((patch // LANES, rows...  5.56 us
    pallas_call x1, Pallas kernels, apply_steps(): pl.pallas_call(apply_kernel, out_shape=pltpu.VMEM(image.shape, F32), in_s...  5.08 us

profile of v3, /device:TPU:1, one launch (start us, length us, event | category | flops | bytes accessed | tf_op | source)
XLA Modules:
  0.0 93.3 jit_solution(11947514067539071619)
XLA Ops:
  0.6 0.0 copy-start
  0.6 0.7 copy-done
  1.3 5.6 %table.1 = (f32[16,80,128]{2,1,0:T(8,128)S(1)}, f32[8,128]{1,0:T(8,128)S(1)}) custom-call(s32[2,32]{1,0:T(2,128)S(1)} %bitcast.1, f32[1,32,16384]{2,1,0:T(8,128)} %res.3, f32[1,64,2048]{2,1,0:T(8,128)} %psf.3), custom_call_target="tpu_custom_call" | custom-call | tf_op jit(solution)/shard_map/table/pallas_call | solution.py:120
  6.9 45.8 %gather.1 = (f32[16,2048,128]{2,1,0:T(8,128)S(1)}, f32[32,8,128]{2,1,0:T(8,128)S(1)}, f32[32,16384]{1,0:T(8,128)S(1)}) custom-call(f32[16,80,128]{2,1,0:T(8,128)S(1)} %get-tuple-element.9.own, f32[8,128]{1,0:T(8,128)S(1)} %get-tuple-element.10.first_part, f32[1,64,2048]{2,1,0:T(8,128)} %psf.3, f32[1,32,16384]{2,1,0:T(8,128)} %res.3), custom_call_target="tpu_custom_call" | custom-call | tf_op jit(solution)/shard_map/gather/pallas_call | solution.py:293
  52.7 5.1 %apply.1.img = f32[32,16384]{1,0:T(8,128)S(1)} custom-call(s32[2,32]{1,0:T(2,128)S(1)} %bitcast.2, f32[32,8,128]{2,1,0:T(8,128)S(1)} %get-tuple-element.11.amps, f32[16,2048,128]{2,1,0:T(8,128)S(1)} %get-tuple-element.12.g, f32[32,16384]{1,0:T(8,128)S(1)} %get-tuple-element.13.given), custom_call_target="tpu_custom_call", output_to_operand_aliasing={{}: (3, {})} | custom-call | tf_op jit(solution)/shard_map/apply/pallas_call | solution.py:352
  57.8 34.0 %reduce.1 = (f32[32,4096]{1,0:T(8,128)S(1)}, f32[8,128]{1,0:T(8,128)S(1)}) custom-call(f32[32,16384]{1,0:T(8,128)S(1)} %apply.1.img), custom_call_target="tpu_custom_call" | custom-call | tf_op jit(solution)/shard_map/reduce/pallas_call | solution.py:455
  91.8 1.5 %write.1 = (f32[1,32,16384]{2,1,0:T(8,128)}, f32[32,4096]{1,0:T(8,128)}) custom-call(f32[32,16384]{1,0:T(8,128)S(1)} %apply.1.img, f32[32,4096]{1,0:T(8,128)S(1)} %get-tuple-element.14.parts, f32[8,128]{1,0:T(8,128)S(1)} %get-tuple-element.15.scale), custom_call_target="tpu_custom_call" | custom-call | tf_op jit(solution)/shard_map/write/pallas_call | solution.py:483
Async XLA Ops:
  0.6 0.7 copy-start

commit v4 on v3

--- a/solution.py
+++ b/solution.py
@@ -14,33 +14,53 @@
 ROWS = ("z", "y", "core")
 MESH = pl.DeviceIdType.MESH
 F32 = jnp.float32
-PIECES = (("z", 1, 0, 4), ("z", -1, 4, 4), ("y", 1, 8, 4), ("y", -1, 12, 4))
-ONE, TWO = (1, 3), (2,)
-ZY, YZ = (0, 1), (2, 3)
-
-
-def order():
-    def both(firsts, seconds):
-        return [
-            item
-            for f in firsts
-            for s in seconds
-            for half in range(2)
-            for item in (((f, s), ZY[half]), ((s, f), YZ[half]))
-        ]
-
-    return [
-        both(ONE, (0,)),
-        both((0,), ONE),
-        both(TWO, (0,)),
-        both(ONE, ONE),
-        both((0,), TWO),
-        both(TWO, ONE),
-        both(ONE, TWO) + both(TWO, TWO),
-    ]
-
-
-def table_kernel(pos, res, psf, own, part, tiles, load_sem, tile_sem):
+PIECES = 4
+PROGRAM = (
+    (65, 265, 269, 268, 193, 194, 73, 273, 277, 196, 209, 210, 529, 137, 473, 533, 138, 475, 476, 457, 513, 321, 281, 141, 459, 276, 201, 202, 521, 345, 337, 525, 460, 217, 218, 537, 385, 449, 285, 387, 212, 129, 130, 451, 81, 393, 541, 284, 145, 146, 325, 395, 89, 465, 349, 467, 153, 154, 409, 329, 257, 341, 401, 403, 0, 0, 0, 0, 0, 0),
+    (36, 44, 52, 60, 97, 289, 101, 225, 226, 228, 121, 305, 293, 233, 308, 105, 481, 125, 483, 241, 242, 236, 113, 313, 309, 169, 170, 484, 441, 377, 317, 443, 425, 427, 316, 489, 161, 297, 381, 433, 435, 497, 292, 361, 353, 249, 505, 177, 369, 185, 417, 0, 0, 0, 0, 0, 0, 0, 0, 0, 0, 0, 0, 0, 0, 0, 0, 0, 0, 0),
+    (69, 68, 77, 76, 137, 321, 141, 84, 129, 345, 325, 92, 265, 145, 329, 349, 324, 193, 194, 217, 385, 389, 348, 218, 473, 475, 529, 153, 337, 85, 332, 273, 521, 524, 201, 449, 451, 93, 340, 457, 537, 276, 393, 257, 459, 333, 209, 513, 401, 409, 281, 465, 0, 0, 0, 0, 0, 0, 0, 0, 0, 0, 0, 0, 0, 0, 0, 0, 0, 0),
+    (101, 108, 125, 116, 33, 161, 361, 41, 162, 109, 100, 49, 177, 353, 178, 57, 117, 124, 185, 441, 186, 443, 225, 445, 444, 226, 425, 417, 427, 305, 165, 308, 419, 545, 169, 553, 170, 233, 365, 555, 234, 689, 241, 505, 690, 507, 481, 181, 242, 561, 433, 369, 483, 313, 314, 569, 249, 377, 435, 250, 289, 497, 489, 297, 491, 0, 0, 0, 0, 0),
+    (141, 132, 133, 148, 65, 201, 393, 202, 149, 156, 73, 217, 385, 218, 221, 396, 81, 209, 449, 210, 451, 157, 388, 89, 473, 465, 475, 474, 585, 205, 588, 601, 321, 193, 401, 467, 602, 577, 397, 580, 593, 457, 409, 345, 194, 459, 405, 329, 265, 521, 266, 523, 257, 337, 513, 273, 529, 281, 537, 0, 0, 0, 0, 0, 0, 0, 0, 0, 0, 0),
+    (165, 172, 181, 188, 105, 241, 433, 242, 189, 436, 113, 249, 425, 250, 429, 164, 97, 489, 497, 491, 173, 180, 121, 225, 417, 499, 226, 245, 108, 441, 233, 361, 234, 437, 116, 481, 369, 305, 483, 545, 253, 420, 505, 364, 289, 353, 507, 561, 493, 372, 377, 297, 553, 313, 569, 0, 0, 0, 0, 0, 0, 0, 0, 0, 0, 0, 0, 0, 0, 0),
+    (196, 205, 212, 221, 129, 457, 460, 213, 145, 473, 204, 477, 265, 266, 153, 401, 220, 197, 273, 393, 257, 132, 461, 529, 531, 530, 385, 449, 148, 269, 137, 513, 514, 585, 465, 587, 156, 261, 521, 601, 523, 522, 577, 409, 602, 404, 579, 281, 285, 578, 329, 537, 539, 593, 321, 345, 337, 0, 0, 0, 0, 0, 0, 0, 0, 0, 0, 0, 0, 0),
+    (228, 245, 234, 250, 236, 253, 226, 242, 169, 489, 491, 244, 493, 185, 497, 499, 172, 229, 97, 433, 425, 434, 428, 237, 289, 161, 481, 483, 561, 562, 436, 485, 121, 177, 553, 555, 252, 293, 505, 305, 105, 297, 188, 313, 617, 113, 633, 635, 625, 417, 377, 569, 441, 361, 353, 369, 545, 609, 0, 0, 0, 0, 0, 0, 0, 0, 0, 0, 0, 0),
+    (267, 261, 260, 258, 275, 277, 284, 266, 337, 537, 473, 475, 285, 540, 274, 329, 529, 449, 283, 333, 268, 282, 193, 393, 513, 465, 209, 339, 341, 276, 338, 321, 521, 457, 451, 541, 476, 330, 137, 577, 585, 385, 395, 532, 450, 201, 601, 217, 467, 460, 657, 409, 345, 129, 259, 401, 665, 641, 593, 145, 649, 153, 0, 0, 0, 0, 0, 0, 0, 0),
+    (291, 301, 300, 290, 307, 317, 308, 314, 353, 553, 481, 483, 557, 556, 298, 377, 569, 497, 315, 357, 572, 306, 225, 633, 545, 489, 379, 637, 500, 354, 361, 561, 417, 299, 293, 292, 418, 241, 441, 369, 505, 355, 309, 484, 498, 609, 233, 169, 365, 617, 433, 371, 492, 442, 381, 425, 434, 613, 161, 177, 249, 625, 185, 0, 0, 0, 0, 0, 0, 0),
+    (341, 323, 348, 322, 346, 333, 324, 347, 257, 393, 585, 394, 397, 332, 331, 281, 385, 577, 330, 325, 340, 387, 537, 401, 593, 402, 581, 588, 339, 265, 449, 601, 338, 260, 451, 273, 409, 521, 413, 193, 284, 259, 217, 473, 665, 513, 540, 411, 465, 529, 641, 201, 657, 457, 649, 209, 0, 0, 0, 0, 0, 0, 0, 0, 0, 0, 0, 0, 0, 0),
+    (370, 357, 364, 363, 378, 381, 372, 355, 297, 441, 633, 362, 637, 356, 443, 305, 417, 609, 161, 354, 365, 380, 419, 553, 433, 617, 177, 298, 445, 636, 555, 569, 505, 625, 185, 442, 613, 612, 507, 437, 497, 425, 673, 225, 306, 620, 371, 165, 434, 289, 697, 561, 169, 572, 379, 181, 506, 233, 629, 498, 481, 681, 689, 299, 189, 241, 489, 545, 313, 249),
+    (410, 397, 404, 395, 388, 389, 387, 386, 345, 449, 665, 396, 405, 451, 394, 321, 465, 641, 412, 453, 467, 402, 201, 329, 457, 657, 348, 413, 403, 346, 721, 217, 337, 705, 209, 649, 668, 669, 411, 330, 644, 585, 729, 713, 469, 458, 324, 473, 205, 660, 257, 273, 593, 338, 661, 724, 577, 601, 213, 588, 281, 513, 193, 521, 537, 529, 265, 0, 0, 0),
+    (428, 445, 435, 434, 420, 421, 427, 418, 361, 497, 697, 444, 437, 499, 426, 369, 505, 689, 700, 509, 419, 442, 241, 353, 481, 681, 692, 429, 363, 482, 249, 377, 297, 701, 371, 362, 561, 633, 313, 507, 354, 225, 625, 355, 609, 489, 378, 379, 673, 233, 299, 617, 553, 315, 545, 569, 289, 305, 0, 0, 0, 0, 0, 0, 0, 0, 0, 0, 0, 0),
+    (453, 476, 459, 466, 469, 475, 452, 458, 401, 705, 257, 461, 403, 468, 474, 385, 729, 273, 709, 259, 460, 450, 393, 713, 281, 733, 451, 388, 402, 409, 649, 329, 265, 277, 467, 386, 345, 348, 337, 411, 394, 665, 529, 641, 668, 537, 331, 321, 644, 513, 657, 721, 593, 521, 585, 601, 577, 0, 0, 0, 0, 0, 0, 0, 0, 0, 0, 0, 0, 0),
+    (501, 491, 484, 506, 509, 499, 500, 490, 233, 425, 737, 249, 297, 485, 427, 492, 482, 225, 417, 745, 241, 313, 301, 483, 420, 498, 441, 673, 553, 317, 555, 508, 426, 697, 753, 353, 493, 299, 236, 418, 433, 545, 428, 689, 761, 633, 677, 635, 442, 561, 681, 252, 557, 569, 289, 443, 354, 549, 617, 305, 293, 361, 362, 625, 355, 309, 377, 369, 609, 0),
+    (524, 530, 539, 533, 531, 517, 514, 516, 793, 257, 585, 785, 721, 515, 525, 522, 540, 769, 265, 777, 705, 523, 541, 538, 796, 321, 273, 465, 587, 797, 586, 724, 345, 281, 601, 657, 589, 722, 532, 603, 641, 337, 409, 789, 410, 468, 659, 577, 393, 329, 457, 460, 401, 403, 473, 449, 665, 593, 595, 649, 385, 651, 713, 729, 0, 0, 0, 0, 0, 0),
+    (555, 565, 546, 556, 571, 573, 570, 564, 289, 625, 745, 547, 549, 746, 548, 633, 313, 753, 609, 563, 629, 754, 572, 297, 761, 369, 557, 554, 292, 371, 305, 737, 617, 373, 562, 748, 619, 353, 505, 377, 637, 626, 316, 489, 417, 673, 361, 613, 418, 756, 481, 381, 634, 497, 681, 762, 441, 433, 425, 689, 697, 0, 0, 0, 0, 0, 0, 0, 0, 0),
+    (602, 588, 587, 589, 579, 596, 578, 321, 521, 657, 325, 595, 580, 594, 345, 513, 641, 349, 603, 516, 522, 769, 393, 537, 649, 645, 523, 524, 538, 777, 329, 793, 665, 397, 515, 324, 658, 586, 401, 721, 713, 405, 643, 540, 650, 385, 785, 666, 669, 337, 529, 409, 651, 796, 722, 389, 714, 465, 705, 457, 729, 473, 449, 0, 0, 0, 0, 0, 0, 0),
+    (635, 620, 610, 629, 611, 612, 626, 637, 613, 369, 553, 673, 619, 556, 634, 373, 377, 561, 681, 627, 628, 562, 809, 621, 361, 545, 761, 675, 636, 762, 825, 381, 353, 569, 689, 563, 372, 365, 297, 289, 737, 683, 828, 801, 441, 745, 697, 547, 305, 817, 481, 313, 433, 425, 505, 489, 753, 497, 417, 0, 0, 0, 0, 0, 0, 0, 0, 0, 0, 0),
+    (660, 667, 642, 661, 650, 652, 643, 645, 409, 585, 713, 586, 412, 659, 653, 385, 593, 721, 857, 594, 668, 723, 669, 651, 393, 577, 705, 833, 666, 644, 717, 715, 401, 513, 729, 514, 596, 389, 601, 595, 413, 345, 521, 529, 714, 580, 579, 709, 836, 515, 329, 321, 465, 777, 706, 523, 733, 841, 844, 531, 457, 537, 473, 793, 449, 337, 785, 769, 849, 0),
+    (690, 676, 699, 677, 698, 684, 691, 685, 433, 617, 761, 674, 620, 683, 765, 417, 609, 737, 682, 692, 693, 425, 553, 561, 563, 618, 700, 741, 441, 625, 569, 627, 554, 436, 809, 481, 633, 489, 485, 801, 570, 361, 369, 745, 493, 817, 610, 353, 825, 753, 634, 497, 505, 377, 545, 0, 0, 0, 0, 0, 0, 0, 0, 0, 0, 0, 0, 0, 0, 0),
+    (717, 724, 730, 707, 706, 708, 725, 731, 465, 657, 529, 714, 468, 709, 715, 457, 649, 513, 722, 660, 733, 651, 777, 473, 409, 521, 658, 412, 533, 449, 665, 537, 666, 460, 469, 857, 401, 641, 793, 642, 652, 477, 849, 385, 593, 595, 585, 732, 577, 601, 393, 833, 785, 769, 841, 0, 0, 0, 0, 0, 0, 0, 0, 0, 0, 0, 0, 0, 0, 0),
+    (738, 748, 765, 739, 746, 756, 741, 747, 505, 673, 561, 562, 764, 565, 675, 489, 681, 569, 506, 740, 573, 755, 801, 481, 617, 545, 817, 618, 508, 493, 547, 763, 497, 689, 625, 754, 676, 749, 683, 873, 571, 425, 697, 553, 762, 684, 757, 619, 809, 627, 417, 433, 369, 546, 692, 509, 825, 371, 690, 549, 441, 633, 700, 353, 865, 609, 377, 881, 361, 889),
+    (772, 781, 795, 787, 789, 780, 771, 779, 529, 849, 530, 853, 532, 513, 841, 514, 517, 788, 729, 521, 601, 522, 603, 773, 796, 897, 537, 577, 538, 579, 797, 516, 705, 473, 475, 585, 593, 457, 597, 708, 713, 595, 721, 833, 845, 905, 715, 409, 641, 410, 857, 385, 657, 449, 913, 393, 665, 465, 921, 649, 401, 0, 0, 0, 0, 0, 0, 0, 0, 0),
+    (805, 812, 821, 828, 545, 865, 813, 548, 569, 881, 829, 804, 737, 745, 889, 869, 820, 753, 609, 489, 490, 491, 573, 572, 481, 553, 873, 497, 498, 483, 885, 740, 561, 689, 505, 506, 441, 893, 748, 425, 427, 756, 625, 673, 697, 613, 417, 418, 433, 681, 633, 617, 761, 0, 0, 0, 0, 0, 0, 0, 0, 0, 0, 0, 0, 0, 0, 0, 0, 0),
+    (853, 860, 845, 836, 601, 769, 897, 771, 605, 604, 577, 777, 905, 779, 581, 580, 593, 529, 641, 530, 597, 844, 521, 785, 913, 522, 787, 837, 772, 537, 793, 921, 538, 645, 532, 657, 513, 729, 585, 514, 661, 540, 473, 475, 649, 705, 665, 796, 721, 449, 451, 465, 466, 713, 457, 0, 0, 0, 0, 0, 0, 0, 0, 0, 0, 0, 0, 0, 0, 0),
+    (869, 876, 885, 868, 609, 809, 929, 811, 893, 812, 625, 825, 937, 827, 613, 628, 633, 545, 689, 546, 877, 548, 561, 801, 697, 690, 803, 441, 693, 884, 761, 817, 673, 562, 699, 425, 677, 892, 819, 569, 681, 570, 427, 417, 685, 828, 945, 419, 553, 737, 497, 498, 745, 505, 753, 953, 617, 481, 433, 489, 0, 0, 0, 0, 0, 0, 0, 0, 0, 0),
+    (900, 901, 909, 908, 961, 641, 857, 969, 859, 645, 860, 977, 649, 833, 835, 985, 917, 916, 585, 601, 586, 603, 729, 925, 604, 602, 593, 577, 578, 777, 733, 924, 779, 594, 449, 665, 841, 785, 652, 843, 473, 513, 769, 514, 451, 465, 469, 849, 836, 713, 529, 530, 787, 721, 771, 457, 705, 537, 538, 851, 657, 793, 521, 0, 0, 0, 0, 0, 0, 0),
+    (933, 932, 941, 940, 689, 873, 693, 876, 697, 865, 701, 700, 737, 673, 809, 811, 677, 948, 801, 681, 625, 803, 685, 628, 817, 819, 489, 617, 545, 546, 949, 956, 561, 562, 497, 499, 501, 553, 881, 554, 676, 957, 745, 569, 889, 570, 684, 621, 753, 481, 609, 825, 633, 761, 505, 0, 0, 0, 0, 0, 0, 0, 0, 0, 0, 0, 0, 0, 0, 0),
+    (965, 973, 981, 989, 729, 897, 732, 777, 779, 733, 705, 905, 900, 785, 708, 781, 713, 857, 859, 849, 716, 789, 721, 913, 851, 513, 514, 908, 853, 657, 601, 603, 602, 769, 860, 725, 665, 921, 771, 793, 529, 916, 661, 641, 649, 593, 594, 585, 668, 833, 924, 841, 521, 652, 577, 537, 0, 0, 0, 0, 0, 0, 0, 0, 0, 0, 0, 0, 0, 0),
+    (737, 929, 740, 741, 801, 803, 745, 937, 805, 817, 819, 489, 492, 561, 873, 562, 875, 821, 809, 497, 500, 505, 697, 811, 506, 565, 825, 508, 617, 945, 827, 618, 749, 865, 481, 700, 753, 625, 867, 626, 757, 569, 620, 570, 553, 761, 953, 765, 881, 883, 545, 546, 673, 689, 889, 891, 681, 609, 610, 633, 0, 0, 0, 0, 0, 0, 0, 0, 0, 0),
+)
+STAGES = (7, 15, 25, 36)
+SOLVE = tuple(range(39, 63, 3))
+
+
+def choose(values, bits):
+    if len(set(values)) == 1:
+        return jnp.int32(values[0])
+    half = len(values) // 2
+    return jnp.where(bits[0], choose(values[half:], bits[1:]), choose(values[:half], bits[1:]))
+
+
+def table_kernel(pos, res, psf, part, own, tiles, load_sem, tile_sem):
     unit = 8 * lax.axis_index("z") + 2 * lax.axis_index("y") + lax.axis_index("core")
     slab = res.shape[1]
     rows = own.shape[1] - 2 * PAD
@@ -119,10 +139,10 @@
     sems = pltpu.SemaphoreType.DMA
     return pl.pallas_call(
         table_kernel,
-        out_shape=(pltpu.VMEM((patch // LANES, rows + 2 * PAD, LANES), F32), pltpu.VMEM((8, LANES), F32)),
+        out_shape=pltpu.VMEM((8, LANES), F32),
         in_specs=[pl.BlockSpec(memory_space=pltpu.SMEM)] + [pl.BlockSpec(memory_space=pltpu.HBM)] * 2,
-        out_specs=(pl.BlockSpec(memory_space=pltpu.VMEM),) * 2,
-        scratch_shapes=[pltpu.VMEM((STEPS, 8, LANES), F32), sems((patch // LANES,)), sems((STEPS,))],
+        out_specs=pl.BlockSpec(memory_space=pltpu.VMEM),
+        scratch_shapes=[pltpu.VMEM((patch // LANES, rows + 2 * PAD, LANES), F32), pltpu.VMEM((STEPS, 8, LANES), F32), sems((patch // LANES,)), sems((STEPS,))],
         compiler_params=pltpu.CompilerParams(vmem_limit_bytes=8 * 1024 * 1024),
         name="table",
     )(positions, pinned(residual, pltpu.HBM), pinned(psf, pltpu.HBM))
@@ -131,12 +151,13 @@
 pinned = pltpu.with_memory_space_constraint
 
 
-def gather_kernel(own, first_part, psf, res, g, amps, img, part, got, table, load_sem, send_sem, recv_sem, peer_send, peer_recv, sum_send, sum_recv):
+def gather_kernel(first_part, psf, res, g, amps, img, part, got, table, load_sem, send_sem, recv_sem, peer_send, peer_recv, sum_send, sum_recv):
     x, z, y, core = (lax.axis_index(a) for a in ("chan",) + ROWS)
     coord = {"z": z, "y": y, "chan": x, "core": core}
     size = {"z": 4, "y": 4, "chan": 4, "core": 2}
-    rows = own.shape[1] - 2 * PAD
-    blocks = own.shape[0]
+    rows = psf.shape[1]
+    blocks = g.shape[0]
+    count = blocks // PIECES
 
     def device(axis, step):
         return {axis: lax.rem(coord[axis] + step % size[axis], size[axis])}
@@ -146,125 +167,48 @@
     for axis, step in greeted:
         pl.semaphore_signal(barrier, inc=1, device_id=device(axis, step), device_id_type=MESH)
 
-    unit = 8 * z + 2 * y + core
+    chip = 4 * z + y
+    unit = 2 * chip + core
+    bits = [((unit >> n) & 1) == 1 for n in (4, 3, 2, 1, 0)]
+    packed = [
+        choose([sum(c << 10 * n for n, c in enumerate(p[t : t + 3])) for p in PROGRAM], bits) for t in range(0, len(PROGRAM[0]), 3)
+    ]
     place_copies = [
         pltpu.make_async_copy(psf.at[0, :, pl.ds(b * LANES, LANES)], g.at[b, pl.ds(unit * rows, rows)], load_sem.at[b])
         for b in range(blocks)
     ]
-    place_copies.append(pltpu.make_async_copy(res.at[0], img, load_sem.at[blocks]))
+    image_copy = pltpu.make_async_copy(res.at[0], img, load_sem.at[blocks])
     for copy in place_copies:
         copy.start()
+    image_copy.start()
+    for copy in place_copies:
+        copy.wait()
     pl.semaphore_wait(barrier, len(greeted))
 
-    def home(d):
-        zh, yh = lax.rem(z + d[0], 4), lax.rem(y + d[1], 4)
-        return 4 * zh + yh
-
-    def needed(h, step_z):
-        row = lax.rem(z + step_z % 4, 4)
-        return jnp.logical_and(h >= 2 * row, h <= 2 * row + 9)
-
-    sends = []
-
-    def forward(d, piece, axis, step, condition):
-        first, _, start, count = PIECES[piece]
-        rel = list(d)
-        rel["zy".index(axis)] = (rel["zy".index(axis)] - step) % 4
-        slot = (rel[0] * 4 + rel[1]) * 4 + piece
-        dst = g.at[pl.ds(start, count), pl.ds((2 * home(d) + core) * rows, rows)]
-        src = own.at[pl.ds(start, count), pl.ds(PAD, rows)] if d == (0, 0) else dst
-        copy = pltpu.make_async_remote_copy(src, dst, send_sem.at[len(sends)], recv_sem.at[slot], device_id=device(axis, step), device_id_type=MESH)
-        pl.when(condition)(copy.start)
-        sends.append((copy, condition))
-
-    def share(d, piece, condition):
-        _, _, start, count = PIECES[piece]
-        slot = (d[0] * 4 + d[1]) * 4 + piece
-        dst = g.at[pl.ds(start, count), pl.ds((2 * home(d) + core) * rows, rows)]
-        src = own.at[pl.ds(start, count), pl.ds(PAD, rows)] if d == (0, 0) else dst
-        copy = pltpu.make_async_remote_copy(src, dst, peer_send.at[slot], peer_recv.at[slot], device_id=device("core", 1), device_id_type=MESH)
-        pl.when(condition)(copy.start)
-        return copy
-
-    shares = []
-
-    def arrived(d, piece, phase=None):
-        first, way, start, count = PIECES[piece]
-        second = "y" if first == "z" else "z"
-        rel = dict(zip("zy", d))
-        h = home(d)
-        here = needed(h, 0)
-        if d != (0, 0):
-            slot = (d[0] * 4 + d[1]) * 4 + piece
-            dst = g.at[pl.ds(start, count), pl.ds((2 * h + core) * rows, rows)]
-            wait = pltpu.make_async_remote_copy(dst, dst, send_sem.at[0], recv_sem.at[slot], device_id=device("core", 1), device_id_type=MESH)
-            pl.when(here)(wait.wait_recv)
-
-        def along(axis, step, also=True):
-            condition = jnp.logical_and(jnp.logical_and(here, needed(h, step)), also) if axis == "z" else here
-            forward(d, piece, axis, step, condition)
-
-        def relay(axis):
-            if axis == "y":
-                if rel["y"] == -way % 4:
-                    along("y", way)
-            elif rel["z"] == 3:
-                along("z", 1, lax.rem(z, 4) == 3)
-            elif rel["z"] == 1:
-                along("z", -1, lax.rem(z, 4) == 0)
-
-        if d == (0, 0):
-            for axis in (first, second) if phase is None else ((first,), (second,))[phase]:
-                along(axis, 1)
-                along(axis, -1)
-            if phase == 0:
-                return
-        elif rel[second] == 0:
-            relay(first)
-            along(second, 1)
-            along(second, -1)
-        else:
-            relay(second)
-        shares.append((share(d, piece, here), here))
-
-    sums = []
-
-    def exchange(axis, value, steps, at):
-        copies = []
-        for n, step in enumerate(steps):
-            copy = pltpu.make_async_remote_copy(
-                part.at[value] if value else first_part, got.at[at + n], sum_send.at[at + n], sum_recv.at[at + n], device_id=device(axis, step), device_id_type=MESH
+    def block(slot):
+        return g.at[pl.ds((slot & 3) * count, count), pl.ds(pl.multiple_of((slot >> 2) * rows, rows), rows)]
+
+    def remote(slot, sems, where):
+        return pltpu.make_async_remote_copy(block(slot), block(slot), *sems, device_id=where, device_id_type=MESH)
+
+    def share(slot):
+        return remote(slot, (peer_send.at[slot], peer_recv.at[slot]), device("core", 1))
+
+    def exchange(n):
+        axis, steps, at = stages[n]
+        return [
+            pltpu.make_async_remote_copy(
+                part.at[n] if n else first_part, got.at[at + m], sum_send.at[at + m], sum_recv.at[at + m], device_id=device(axis, step), device_id_type=MESH
             )
-            copies.append(copy)
-        return copies
-
-    waves = order()
-    stages = [("core", (1,), 0), ("y", (1, 2, 3), 1), ("z", (1, 2, 3), 4), ("chan", (3, 2, 1), 7)]
-    after = ([], waves[0], waves[1] + waves[2], waves[3])
-    for n, (axis, steps, at) in enumerate(stages):
-        copies = exchange(axis, n, steps, at)
-        for copy in copies:
-            copy.start()
-        if n == 0:
-            for piece in range(4):
-                arrived((0, 0), piece, 0)
-        if n == 1:
-            for piece in range(4):
-                arrived((0, 0), piece, 1)
-        for d, piece in after[n]:
-            arrived(d, piece)
-        for copy in copies:
-            copy.wait()
-        if axis != "chan":
-            part[n + 1] = sum((got[at + m] for m in range(len(steps))), part[n] if n else first_part[...])
-    for wave in waves[4:6]:
-        for d, piece in wave:
-            arrived(d, piece)
-    tables = [part[3]] + [got[7 + m] for m in range(3)]
-    for i in range(STEPS // 4):
-        rows_of = jnp.concatenate([t[i : i + 1, :] for t in tables] + [jnp.zeros((4, LANES), F32)], axis=0)
-        for m in range(4):
-            table[4 * i + m] = rows_of if m == 0 else pltpu.roll(rows_of, LANES - LANES // 4 * m, 1)
+            for m, step in enumerate(steps)
+        ]
+
+    def spread():
+        tables = [part[3]] + [got[7 + m] for m in range(3)]
+        for i in range(STEPS // 4):
+            rows_of = jnp.concatenate([t[i : i + 1, :] for t in tables] + [jnp.zeros((4, LANES), F32)], axis=0)
+            for m in range(4):
+                table[4 * i + m] = rows_of if m == 0 else pltpu.roll(rows_of, LANES - LANES // 4 * m, 1)
 
     wide = lax.broadcasted_iota(jnp.int32, (8, LANES), 1)
 
@@ -274,42 +218,78 @@
         amps[j] = jnp.broadcast_to(amp[0:1, :], (8, LANES))
         return left - amp * table[j]
 
-    lax.fori_loop(0, STEPS, solve, table[STEPS - 1])
-
-    for d, piece in waves[6]:
-        arrived(d, piece)
-    for copy in place_copies:
-        copy.wait()
-    for copy, condition in shares:
-        pl.when(condition)(copy.wait)
-    for copy, condition in sends:
-        pl.when(condition)(copy.wait_send)
-
-
-def gather(own, part, psf, residual):
+    stages = [("core", (1,), 0), ("y", (1, 2, 3), 1), ("z", (1, 2, 3), 4), ("chan", (3, 2, 1), 7)]
+    copies = exchange(0)
+    for copy in copies:
+        copy.start()
+    for piece in range(PIECES):
+        share(unit * PIECES + piece).start()
+    sends = []
+    for t in range(len(PROGRAM[0])):
+        if t in STAGES:
+            n = STAGES.index(t)
+            for copy in copies:
+                copy.wait()
+            if n < 3:
+                _, steps, at = stages[n]
+                part[n + 1] = sum((got[at + m] for m in range(len(steps))), part[n] if n else first_part[...])
+                copies = exchange(n + 1)
+                for copy in copies:
+                    copy.start()
+            else:
+                spread()
+                left = table[STEPS - 1]
+        if t in SOLVE:
+            j = STEPS // len(SOLVE) * SOLVE.index(t)
+            left = lax.fori_loop(j, j + STEPS // len(SOLVE), solve, left)
+        code = packed[t // 3] >> 10 * (t % 3)
+        kind, slot = code & 7, (code >> 3) & 127
+        up = jnp.where(kind == 2, 1, jnp.where(kind == 3, 3, 0))
+        over = jnp.where(kind == 4, 1, jnp.where(kind == 5, 3, 0))
+        copy = remote(slot, (send_sem.at[t], recv_sem.at[slot]), {"z": (z + up) & 3, "y": (y + over) & 3})
+        shard = slot >> 2
+        mine = share(slot)
+        if any(p[t] % 8 == 1 for p in PROGRAM):
+            pl.when(kind == 1)(copy.wait_recv)
+            pl.when((kind == 1) & (shard >= chip) & (shard <= chip + 16))(mine.start)
+        if any(p[t] % 8 > 1 for p in PROGRAM):
+            pl.when(kind > 1)(copy.start)
+            sends.append((kind > 1, copy))
+    image_copy.wait()
+    for n in range(9):
+        for piece in range(PIECES):
+            theirs = chip + ((chip + 1 - core) & 1) + 2 * n
+            ours = chip + ((chip + core) & 1) + 2 * n
+            pl.when(theirs <= chip + 16)(share(theirs * PIECES + piece).wait_recv)
+            pl.when(ours <= chip + 16)(share(ours * PIECES + piece).wait_send)
+    for sent, copy in sends:
+        pl.when(sent)(copy.wait_send)
+
+
+def gather(part, psf, residual):
     patch = psf.shape[2]
     blocks = patch // LANES
     sems = pltpu.SemaphoreType.DMA
     return pl.pallas_call(
         gather_kernel,
         out_shape=(pltpu.VMEM((blocks, patch, LANES), F32), pltpu.VMEM((STEPS, 8, LANES), F32), pltpu.VMEM(residual.shape[1:], F32)),
-        in_specs=[pl.BlockSpec(memory_space=pltpu.VMEM)] * 2 + [pl.BlockSpec(memory_space=pltpu.HBM)] * 2,
+        in_specs=[pl.BlockSpec(memory_space=pltpu.VMEM)] + [pl.BlockSpec(memory_space=pltpu.HBM)] * 2,
         out_specs=(pl.BlockSpec(memory_space=pltpu.VMEM),) * 3,
         scratch_shapes=[
             pltpu.VMEM((4, 8, LANES), F32),
             pltpu.VMEM((10, 8, LANES), F32),
             pltpu.VMEM((STEPS, 8, LANES), F32),
             sems((blocks + 1,)),
-            sems((128,)),
-            sems((64,)),
-            sems((64,)),
-            sems((64,)),
+            sems((len(PROGRAM[0]),)),
+            sems((32 * PIECES,)),
+            sems((32 * PIECES,)),
+            sems((32 * PIECES,)),
             sems((10,)),
             sems((10,)),
         ],
         compiler_params=pltpu.CompilerParams(collective_id=0, has_side_effects=True, vmem_limit_bytes=8 * 1024 * 1024),
         name="gather",
-    )(pinned(own, pltpu.VMEM), pinned(part, pltpu.VMEM), pinned(psf, pltpu.HBM), pinned(residual, pltpu.HBM))
+    )(pinned(part, pltpu.VMEM), pinned(psf, pltpu.HBM), pinned(residual, pltpu.HBM))
 
 
 def apply_kernel(pos, amps, g, given, img):
@@ -327,25 +307,33 @@
         tail = lane >= shift
         amp = amps[k]
         before = [jnp.zeros((8, LANES), F32)] * groups
-        terms = []
-        for j in range(blocks + 1):
-            if j < blocks:
-                now = [pltpu.roll(g[j, pl.ds(start + 8 * i, 8), :] * amp, shift, 1) for i in range(groups)]
-            else:
-                now = [jnp.zeros((8, LANES), F32)] * groups
-            terms.append([jnp.where(tail, n, b) for n, b in zip(now, before)])
-            before = now
-        for j0 in range(0, blocks + 1, 4):
-            js = range(j0, min(j0 + 4, blocks + 1))
-            cols = [jnp.minimum(block + j, ncols // LANES - 1) if j == blocks else block + j for j in js]
-            at = [pl.ds(pl.multiple_of(col * LANES, LANES), LANES) for col in cols]
-            old = [[img[8 * i : 8 * i + 8, a] for i in range(groups)] for a in at]
-            for j, a, o in zip(js, at, old):
+
+        def columns(j):
+            col = jnp.minimum(block + j, ncols // LANES - 1) if j == blocks else block + j
+            return pl.ds(pl.multiple_of(col * LANES, LANES), LANES)
+
+        def subtract(terms):
+            old = [[img[8 * i : 8 * i + 8, columns(j)] for i in range(groups)] for j, _ in terms]
+            for (j, term), o in zip(terms, old):
                 for i in range(groups):
-                    img[8 * i : 8 * i + 8, a] = o[i] - terms[j][i]
+                    img[8 * i : 8 * i + 8, columns(j)] = o[i] - term[i]
+
+        pending = []
+        for js in [range(j, j + 4) for j in range(0, blocks, 4)] + [[blocks]]:
+            terms = []
+            for j in js:
+                if j < blocks:
+                    now = [pltpu.roll(g[j, pl.ds(start + 8 * i, 8), :] * amp, shift, 1) for i in range(groups)]
+                else:
+                    now = [jnp.zeros((8, LANES), F32)] * groups
+                terms.append((j, [jnp.where(tail, n, b) for n, b in zip(now, before)]))
+                before = now
+            subtract(pending)
+            pending = terms
+        subtract(pending)
         return carry
 
-    lax.fori_loop(0, STEPS, step, 0)
+    lax.fori_loop(0, STEPS, step, 0, unroll=4)
 
 
 def apply_steps(positions, amps, g, image):
@@ -493,8 +481,8 @@
 
 def on_device(residual, psf, positions):
     positions = positions.T
-    own, part = peak_table(positions, residual, psf)
-    g, amps, image = gather(own, part, psf, residual)
+    part = peak_table(positions, residual, psf)
+    g, amps, image = gather(part, psf, residual)
     image = apply_steps(positions, amps, g, image)
     parts, scale = reduce_channels(image)
     return write(image, parts, scale)

time: 93.6 us -> 93.4 us (level)
    pallas_call x1, Pallas kernels: 5.08 us -> 3.54 us  [apply_steps(): pl.pallas_call(apply_kernel, out_shape=pltpu.VMEM(image.shape, F32), in_s...]
    pallas_call x1, Pallas kernels: 34 us -> 35 us  [reduce_channels(): pl.pallas_call(reduce_kernel, out_shape=(pltpu.VMEM((slab, width), F32),...]
where the time goes in v4:
time: 93.4 us; the launch traced here: 93.1 us
  Pallas kernels  91.8 us (98%)
    pallas_call x1, Pallas kernels, gather(): pl.pallas_call(gather_kernel, out_shape=(pltpu.VMEM((blocks, patch, LANES...  46.4 us
    pallas_call x1, Pallas kernels, reduce_channels(): pl.pallas_call(reduce_kernel, out_shape=(pltpu.VMEM((slab, width), F32),...  35 us
    pallas_call x1, Pallas kernels, peak_table(): pl.pallas_call(table_kernel, out_shape=pltpu.VMEM((8, LANES), F32), in_sp...  5.39 us
    pallas_call x1, Pallas kernels, apply_steps(): pl.pallas_call(apply_kernel, out_shape=pltpu.VMEM(image.shape, F32), in_s...  3.54 us

profile of v4, /device:TPU:1, one launch (start us, length us, event | category | flops | bytes accessed | tf_op | source)
XLA Modules:
  0.0 93.1 jit_solution(15536627092042252617)
XLA Ops:
  0.6 0.0 copy-start
  0.6 0.7 copy-done
  1.3 5.4 %table.1.first_part = f32[8,128]{1,0:T(8,128)S(1)} custom-call(s32[2,32]{1,0:T(2,128)S(1)} %bitcast.1, f32[1,32,16384]{2,1,0:T(8,128)} %res.3, f32[1,64,2048]{2,1,0:T(8,128)} %psf.3), custom_call_target="tpu_custom_call" | custom-call | tf_op jit(solution)/shard_map/table/pallas_call | solution.py:140
  6.7 46.4 %gather.1 = (f32[16,2048,128]{2,1,0:T(8,128)S(1)}, f32[32,8,128]{2,1,0:T(8,128)S(1)}, f32[32,16384]{1,0:T(8,128)S(1)}) custom-call(f32[8,128]{1,0:T(8,128)S(1)} %table.1.first_part, f32[1,64,2048]{2,1,0:T(8,128)} %psf.3, f32[1,32,16384]{2,1,0:T(8,128)} %res.3), custom_call_target="tpu_custom_call" | custom-call | tf_op jit(solution)/shard_map/gather/pallas_call | solution.py:273
  53.1 3.5 %apply.1.img = f32[32,16384]{1,0:T(8,128)S(1)} custom-call(s32[2,32]{1,0:T(2,128)S(1)} %bitcast.2, f32[32,8,128]{2,1,0:T(8,128)S(1)} %get-tuple-element.7.amps, f32[16,2048,128]{2,1,0:T(8,128)S(1)} %get-tuple-element.8.g, f32[32,16384]{1,0:T(8,128)S(1)} %get-tuple-element.9.given), custom_call_target="tpu_custom_call", output_to_operand_aliasing={{}: (3, {})} | custom-call | tf_op jit(solution)/shard_map/apply/pallas_call | solution.py:340
  56.6 35.0 %reduce.1 = (f32[32,4096]{1,0:T(8,128)S(1)}, f32[8,128]{1,0:T(8,128)S(1)}) custom-call(f32[32,16384]{1,0:T(8,128)S(1)} %apply.1.img), custom_call_target="tpu_custom_call" | custom-call | tf_op jit(solution)/shard_map/reduce/pallas_call | solution.py:443
  91.6 1.5 %write.1 = (f32[1,32,16384]{2,1,0:T(8,128)}, f32[32,4096]{1,0:T(8,128)}) custom-call(f32[32,16384]{1,0:T(8,128)S(1)} %apply.1.img, f32[32,4096]{1,0:T(8,128)S(1)} %get-tuple-element.10.parts, f32[8,128]{1,0:T(8,128)S(1)} %get-tuple-element.11.scale), custom_call_target="tpu_custom_call" | custom-call | tf_op jit(solution)/shard_map/write/pallas_call | solution.py:471
Async XLA Ops:
  0.6 0.7 copy-start
